TPU v7x, 32 devices: a whole 2x2x4 slice. The times are simulated.
32 devices in a mesh: gx: 4 (over z), gy: 2 (over x), gz: 4 (over y, core).
Axes of the slice: x: 2, y: 2, z: 4, core: 2. Of those that a mesh axis runs over, the one named last changes fastest.
Arguments:
- volume: bfloat16 [32, 8, 32, 512], P(None, 'gx', 'gy', 'gz'), may hold values from -6 to 6
- w_first: bfloat16 [3, 3, 3, 32, 32], replicated, may hold values from -0.21875 to 0.21875
- w_second: bfloat16 [3, 3, 3, 32, 32], replicated, may hold values from -0.21875 to 0.21875
- v_first: bfloat16 [3, 3, 3, 32, 32], replicated, may hold values from -0.21875 to 0.21875
- v_second: bfloat16 [3, 3, 3, 32, 32], replicated, may hold values from -0.21875 to 0.21875
Outputs:
- jv: bfloat16 [32, 8, 32, 512], P(None, 'gx', 'gy', 'gz')
- gv_first: float32 [3, 3, 3, 32, 32], replicated
- gv_second: float32 [3, 3, 3, 32, 32], replicated
All inputs are finite; a program needn't handle non-finite values.
Results may differ from a plain program's by a relative error of at most 0.005.
Values may be sent and summed in bfloat16 or wider, within the bound.
A program may use at most 64 MiB of HBM per device.

v0:
```python
import math

import jax
import jax.numpy as jnp
from jax import lax
from jax.sharding import PartitionSpec as P


def padded_2(cells, sides, width):
    for axis, dim in sides:
        count = lax.axis_size(axis)
        ends = count - 1
        head = lax.slice_in_dim(cells, 0, width, axis=dim)
        tail = lax.slice_in_dim(cells, cells.shape[dim] - width, cells.shape[dim], axis=dim)
        cells = jnp.concatenate(
            [
                lax.ppermute(tail, axis, [(i, (i + 1) % count) for i in range(ends)]),
                cells,
                lax.ppermute(head, axis, [((i + 1) % count, i) for i in range(ends)]),
            ],
            axis=dim,
        )
    return cells


def gelu_pair(pre):
    inner = 0.7978845608 * (pre + 0.044715 * pre * pre * pre)
    hyper = jnp.tanh(inner)
    hidden = 0.5 * pre * (1.0 + hyper)
    slope = 0.5 * (1.0 + hyper) + 0.5 * pre * (1.0 - hyper * hyper) * 0.7978845608 * (
        1.0 + 0.134145 * pre * pre
    )
    return (hidden, slope)


def stencil(padded, weight):
    depth = padded.shape[1] - 2
    height = padded.shape[2] - 2
    width = padded.shape[3] - 2
    in_chan = weight.shape[3]
    out_chan = weight.shape[4]
    summed = jnp.zeros((out_chan, depth, height, width), jnp.float32)
    for shift_x in range(3):
        for shift_y in range(3):
            stacked = jnp.concatenate(
                [
                    padded[
                        :,
                        shift_x : shift_x + depth,
                        shift_y : shift_y + height,
                        shift_z : shift_z + width,
                    ]
                    for shift_z in range(3)
                ],
                axis=0,
            )
            matrix = weight[shift_x, shift_y].reshape(3 * in_chan, out_chan)
            summed = summed + jnp.einsum(
                "kxyz,ko->oxyz", stacked, matrix, preferred_element_type=jnp.float32
            )
    return summed


def correlate(padded, target):
    depth = target.shape[1]
    height = target.shape[2]
    width = target.shape[3]
    in_chan = padded.shape[0]
    out_chan = target.shape[0]
    planes = []
    for shift_x in range(3):
        rows_y = []
        for shift_y in range(3):
            stacked = jnp.concatenate(
                [
                    padded[
                        :,
                        shift_x : shift_x + depth,
                        shift_y : shift_y + height,
                        shift_z : shift_z + width,
                    ]
                    for shift_z in range(3)
                ],
                axis=0,
            )
            product = jnp.einsum(
                "kxyz,oxyz->ko", stacked, target, preferred_element_type=jnp.float32
            )
            rows_y.append(product.reshape(3, in_chan, out_chan))
        planes.append(jnp.stack(rows_y))
    return jnp.stack(planes)


def body(volume, w_first, w_second, v_first, v_second):
    channels = volume.shape[0]
    depth = volume.shape[1]
    height = volume.shape[2]
    width = volume.shape[3]
    count_all = float(
        depth * height * width * lax.axis_size("gx") * lax.axis_size("gy") * lax.axis_size("gz")
    )
    factor = math.sqrt(27.0 * channels)
    input_pad = padded_2(volume, (("gx", 1), ("gy", 2), ("gz", 3)), 1)
    pre = stencil(input_pad, w_first)
    hidden_f, slope = gelu_pair(pre)
    hidden = hidden_f.astype(jnp.bfloat16)
    tangent = (slope * stencil(input_pad, v_first)).astype(jnp.bfloat16)
    paired = padded_2(jnp.stack([hidden, tangent]), (("gx", 2), ("gy", 3), ("gz", 4)), 1)
    hidden_pad = paired[0]
    tangent_pad = paired[1]
    jv = (stencil(tangent_pad, w_second) + stencil(hidden_pad, v_second)).astype(jnp.bfloat16)
    local_second = correlate(hidden_pad, jv)
    jv_pad = padded_2(jv, (("gx", 1), ("gy", 2), ("gz", 3)), 1)
    flipped = jnp.transpose(jnp.flip(w_second, (0, 1, 2)), (0, 1, 2, 4, 3))
    back = (slope * stencil(jv_pad, flipped)).astype(jnp.bfloat16)
    local_first = correlate(input_pad, back)
    summed_first, summed_second = lax.psum((local_first, local_second), ("gx", "gy", "gz"))
    gv_first = factor * (summed_first / count_all + 0.1 * v_first.astype(jnp.float32))
    gv_second = factor * (summed_second / count_all + 0.1 * v_second.astype(jnp.float32))
    return (jv, gv_first, gv_second)


def solution(mesh):
    in_specs = (P(None, "gx", "gy", "gz"), P(), P(), P(), P())
    out_specs = (P(None, "gx", "gy", "gz"), P(), P())
    return jax.shard_map(body, mesh=mesh, in_specs=in_specs, out_specs=out_specs, check_vma=False)
```

profile of v0, /device:TPU:0, one launch (start us, length us, event | category | flops | bytes accessed | tf_op | source)
XLA Modules:
  0.0 293.0 jit_solution(8699240827730390942)
XLA Ops:
  7.2 1.1 copy.134
  8.4 1.3 collective-permute-start.1
  9.7 5.6 %collective-permute-start = (bf16[32,1,16,128]{3,0,2,1:T(8,128)(2,1)S(1)}, bf16[32,1,16,128]{3,0,2,1:T(8,128)(2,1)S(1)}, u32[]{:S(2)}, u32[]{:S(2)}) collective-permute-start(bf16[32,1,16,128]{3,0,2,1:T(8,128)(2,1)S(1)} %get-tuple-element.141), channel_id=1, source_target_pairs={{0,8},{8,16},{16,24},{1,9},{9,17},{17,25},{2,10},{10,18},{18,26},{... | collective-permute-start | bytes 393224 | tf_op jit(solution)/shard_map/ppermute | solution.py:17
  15.3 1.5 fusion.203
  16.8 1.2 collective-permute-done
  18.2 3.6 %collective-permute-start.2 = (bf16[32,4,1,128]{3,0,2,1:T(8,128)(2,1)S(1)}, bf16[32,4,1,128]{3,0,2,1:T(8,128)(2,1)S(1)}, u32[]{:S(2)}, u32[]{:S(2)}) collective-permute-start(bf16[32,4,1,128]{3,0,2,1:T(8,128)(2,1)S(1)} %get-tuple-element.136), channel_id=1, source_target_pairs={{0,4},{1,5},{2,6},{3,7},{8,12},{9,13},{10,14},{11,15},{16,20},{17,... | collective-permute-start | bytes 98312 | tf_op jit(solution)/shard_map/ppermute | solution.py:17
  21.8 1.3 collective-permute-start.3
  23.1 0.7 fusion.204
  23.8 3.8 %collective-permute-done.3 = bf16[32,4,1,128]{3,0,2,1:T(8,128)(2,1)S(1)} collective-permute-done((bf16[32,4,1,128]{3,0,2,1:T(8,128)(2,1)S(1)}, bf16[32,4,1,128]{3,0,2,1:T(8,128)(2,1)S(1)}, u32[]{:S(2)}, u32[]{:S(2)}) %collective-permute-start.3) | collective-permute-done | bytes 32800 | tf_op jit(solution)/shard_map/ppermute | solution.py:19
  28.0 1.1 copy.137
  29.6 1.3 collective-permute-start.5
  30.9 3.0 %collective-permute-start.4 = (bf16[32,4,18,1]{0,1,3,2:T(4,128)(2,1)}, bf16[32,4,18,1]{0,1,3,2:T(4,128)(2,1)S(1)}, u32[]{:S(2)}, u32[]{:S(2)}) collective-permute-start(bf16[32,4,18,1]{0,1,3,2:T(4,128)(2,1)} %copy.137), channel_id=1, source_target_pairs={{0,1},{1,2},{2,3},{4,5},{5,6},{6,7},{8,9},{9,10},{10,11},{12,13},{... | collective-permute-start | bytes 13832 | tf_op jit(solution)/shard_map/ppermute | solution.py:17
  34.0 0.9 collective-permute-done.4
  35.5 1.3 copy.140
  36.7 0.8 maximum_maximum_fusion
  37.6 1.1 fusion.191
  46.5 4.3 %collective-permute-start.6 = (bf16[2,32,1,16,128]{4,1,3,2,0:T(8,128)(2,1)S(1)}, bf16[2,32,1,16,128]{4,1,3,2,0:T(8,128)(2,1)S(1)}, u32[]{:S(2)}, u32[]{:S(2)}) collective-permute-start(bf16[2,32,1,16,128]{4,1,3,2,0:T(8,128)(2,1)S(1)} %get-tuple-element.132), channel_id=1, source_target_pairs={{0,8},{8,16},{16,24},{1,9},{9,17},{17,25},{2,10},{10,18},{18,26},{... | collective-permute-start | bytes 786440 | tf_op jit(solution)/shard_map/ppermute | solution.py:17
  50.8 1.3 collective-permute-start.7
  52.2 0.7 fusion.202
  52.9 4.4 %collective-permute-done.6 = bf16[2,32,1,16,128]{4,1,3,2,0:T(8,128)(2,1)S(1)} collective-permute-done((bf16[2,32,1,16,128]{4,1,3,2,0:T(8,128)(2,1)S(1)}, bf16[2,32,1,16,128]{4,1,3,2,0:T(8,128)(2,1)S(1)}, u32[]{:S(2)}, u32[]{:S(2)}) %collective-permute-start.6) | collective-permute-done | bytes 262176 | tf_op jit(solution)/shard_map/ppermute | solution.py:17
  57.3 4.6 %collective-permute-done.7 = bf16[2,32,1,16,128]{4,1,3,2,0:T(8,128)(2,1)S(1)} collective-permute-done((bf16[2,32,1,16,128]{4,1,3,2,0:T(8,128)(2,1)S(1)}, bf16[2,32,1,16,128]{4,1,3,2,0:T(8,128)(2,1)S(1)}, u32[]{:S(2)}, u32[]{:S(2)}) %collective-permute-start.7) | collective-permute-done | bytes 262176 | tf_op jit(solution)/shard_map/ppermute | solution.py:19
  61.9 1.6 collective-permute-start.8
  63.5 1.3 collective-permute-start.9
  64.8 0.7 fusion.200
  65.5 4.1 %collective-permute-done.9 = bf16[2,32,4,1,128]{4,1,3,2,0:T(8,128)(2,1)S(1)} collective-permute-done((bf16[2,32,4,1,128]{4,1,3,2,0:T(8,128)(2,1)S(1)}, bf16[2,32,4,1,128]{4,1,3,2,0:T(8,128)(2,1)S(1)}, u32[]{:S(2)}, u32[]{:S(2)}) %collective-permute-start.9) | collective-permute-done | bytes 65568 | tf_op jit(solution)/shard_map/ppermute | solution.py:19
  69.7 0.6 copy-done.12
  71.1 1.5 copy.162
  72.7 0.9 copy.163
  73.6 1.3 collective-permute-start.11
  74.9 3.2 %collective-permute-start.10 = (bf16[2,32,4,18,1]{1,2,4,3,0:T(4,128)(2,1)}, bf16[2,32,4,18,1]{1,2,4,3,0:T(4,128)(2,1)S(1)}, u32[]{:S(2)}, u32[]{:S(2)}) collective-permute-start(bf16[2,32,4,18,1]{1,2,4,3,0:T(4,128)(2,1)} %copy.162), channel_id=1, source_target_pairs={{0,1},{1,2},{2,3},{4,5},{5,6},{6,7},{8,9},{9,10},{10,11},{12,13},{... | collective-permute-start | bytes 27656 | tf_op jit(solution)/shard_map/ppermute | solution.py:17
  78.1 1.6 fusion.201
  80.0 0.7 reshape.48
  80.7 0.7 reshape.47
  81.4 0.7 reshape.46
  82.1 0.7 reshape.45
  82.8 0.7 reshape.44
  83.5 0.7 reshape.43
  84.2 0.7 reshape.42
  84.9 1.0 copy.164
  85.9 1.7 copy.165
  87.6 3.8 %pad_maximum_fusion = bf16[2,32,4,18,130]{4,1,3,2,0:T(8,128)(2,1)S(1)} fusion(bf16[2,32,4,18,1]{4,1,3,2,0:T(8,128)(2,1)S(1)} %copy.165, bf16[2,32,4,1,128]{4,1,3,2,0:T(8,128)(2,1)} %copy-done.12, bf16[2,32,1,16,128]{4,1,3,2,0:T(8,128)(2,1)} %copy-done.1, bf16[1,32,2,16,128]{4,1,3,2,0:T(8,128)(2,1)S(1)} %fusion.10, bf16[1,32,2,16,128]{4,1,3,2,0:T(8,128)(2,1)S(1)} %fusion.124, ...), kind=kLoop, calls=%fused_computation | loop fusion | flops 9584640 | bytes 2396160 | tf_op jit(solution)/shard_map/concatenate | solution.py:15
  92.2 1.2 fusion.188
  93.9 1.2 fusion.186
  106.1 3.5 %collective-permute-start.12 = (bf16[32,1,16,128]{3,0,2,1:T(8,128)(2,1)S(1)}, bf16[32,1,16,128]{3,0,2,1:T(8,128)(2,1)S(1)}, u32[]{:S(2)}, u32[]{:S(2)}) collective-permute-start(bf16[32,1,16,128]{3,0,2,1:T(8,128)(2,1)S(1)} %get-tuple-element.138), channel_id=1, source_target_pairs={{0,8},{8,16},{16,24},{1,9},{9,17},{17,25},{2,10},{10,18},{18,26},{... | collective-permute-start | bytes 393224 | tf_op jit(solution)/shard_map/ppermute | solution.py:17
  109.6 1.3 collective-permute-start.13
  111.4 2.0 collective-permute-done.12
  113.4 4.1 %collective-permute-done.13 = bf16[32,1,16,128]{3,0,2,1:T(8,128)(2,1)S(1)} collective-permute-done((bf16[32,1,16,128]{3,0,2,1:T(8,128)(2,1)S(1)}, bf16[32,1,16,128]{3,0,2,1:T(8,128)(2,1)S(1)}, u32[]{:S(2)}, u32[]{:S(2)}) %collective-permute-start.13) | collective-permute-done | bytes 131104 | tf_op jit(solution)/shard_map/ppermute | solution.py:19
  117.5 1.6 collective-permute-start.14
  119.1 1.5 collective-permute-start.15
  120.6 1.0 pad_maximum_fusion.27
  121.6 3.3 %collective-permute-done.15 = bf16[32,4,1,128]{3,0,2,1:T(8,128)(2,1)S(1)} collective-permute-done((bf16[32,4,1,128]{3,0,2,1:T(8,128)(2,1)S(1)}, bf16[32,4,1,128]{3,0,2,1:T(8,128)(2,1)S(1)}, u32[]{:S(2)}, u32[]{:S(2)}) %collective-permute-start.15) | collective-permute-done | bytes 32800 | tf_op jit(solution)/shard_map/ppermute | solution.py:19
  126.3 1.3 collective-permute-start.17
  127.6 3.0 %collective-permute-start.16 = (bf16[32,4,18,1]{0,1,3,2:T(4,128)(2,1)S(1)}, bf16[32,4,18,1]{0,1,3,2:T(4,128)(2,1)S(1)}, u32[]{:S(2)}, u32[]{:S(2)}) collective-permute-start(bf16[32,4,18,1]{0,1,3,2:T(4,128)(2,1)S(1)} %copy.184), channel_id=1, source_target_pairs={{0,1},{1,2},{2,3},{4,5},{5,6},{6,7},{8,9},{9,10},{10,11},{12,13},{... | collective-permute-start | bytes 13832 | tf_op jit(solution)/shard_map/ppermute | solution.py:17
  130.9 0.9 fusion.196
  132.9 1.4 maximum_maximum_fusion.1
  134.7 0.7 fusion.185
  138.7 0.8 copy-done.11
  145.4 0.6 copy-done.34
  150.3 1.0 pad_maximum_fusion.26
  151.8 0.8 copy.199
  152.6 129.9 %all-reduce.3.cloned.1.call-done = (f32[3,3,3,32,32]{3,2,4,1,0:T(4,128)}, f32[3,3,3,32,32]{3,2,4,1,0:T(4,128)}) async-done(((f32[3,3,3,32,32]{3,2,4,1,0:T(4,128)}, f32[3,3,3,32,32]{3,2,4,1,0:T(4,128)}), (f32[3,3,3,32,32]{3,2,4,1,0:T(4,128)}, f32[3,3,3,32,32]{3,2,4,1,0:T(4,128)})) %all-reduce.3.cloned.1.call-update) | async-done | bytes 221200 | tf_op jit(solution)/shard_map/psum | solution.py:117
  282.5 1.4 add_multiply_fusion.1
  283.9 1.0 copy.200
  285.2 1.0 copy.201
  (353 shorter events, 39.8 us)
Async XLA Ops:
  7.2 10.9 %copy-start.2 = (bf16[32,2,16,128]{3,2,1,0:T(8,128)(2,1)S(1)}, bf16[32,2,16,128]{3,2,1,0:T(8,128)(2,1)}, u32[]{:S(2)}) copy-start(bf16[32,2,16,128]{3,2,1,0:T(8,128)(2,1)} %param.5) | copy-start | bytes 786436
  7.2 16.0 %copy-start.6 = (bf16[3,3,3,32,32]{4,3,2,1,0:T(8,128)(2,1)S(1)}, bf16[3,3,3,32,32]{4,3,2,1,0:T(8,128)(2,1)}, u32[]{:S(2)}) copy-start(bf16[3,3,3,32,32]{4,3,2,1,0:T(8,128)(2,1)} %param.8) | copy-start | bytes 165892
  7.2 275.3 %all-reduce.3.cloned.1.call-start = ((), (), s32[]{:S(2)}) async-start(), calls=%async_computation | async-start | bytes 2359296 | tf_op jit(solution)/shard_map/psum | solution.py:117
  8.3 37.2 %copy-start.3 = (bf16[32,2,16,128]{3,0,2,1:T(8,128)(2,1)}, bf16[32,2,16,128]{3,0,2,1:T(8,128)(2,1)S(1)}, u32[]{:S(2)}) copy-start(bf16[32,2,16,128]{3,0,2,1:T(8,128)(2,1)S(1)} %copy.134) | copy-start | bytes 786436
  8.4 9.8 %collective-permute-start.1 = (bf16[32,1,16,128]{3,0,2,1:T(8,128)(2,1)S(1)}, bf16[32,1,16,128]{3,0,2,1:T(8,128)(2,1)S(1)}, u32[]{:S(2)}, u32[]{:S(2)}) collective-permute-start(bf16[32,1,16,128]{3,0,2,1:T(8,128)(2,1)S(1)} %get-tuple-element.140), channel_id=1, source_target_pairs={{8,0},{16,8},{24,16},{9,1},{17,9},{25,17},{10,2},{18,10},{26,18},{... | collective-permute-start | bytes 393224 | tf_op jit(solution)/shard_map/ppermute | solution.py:19
  9.7 8.3 %collective-permute-start = (bf16[32,1,16,128]{3,0,2,1:T(8,128)(2,1)S(1)}, bf16[32,1,16,128]{3,0,2,1:T(8,128)(2,1)S(1)}, u32[]{:S(2)}, u32[]{:S(2)}) collective-permute-start(bf16[32,1,16,128]{3,0,2,1:T(8,128)(2,1)S(1)} %get-tuple-element.141), channel_id=1, source_target_pairs={{0,8},{8,16},{16,24},{1,9},{9,17},{17,25},{2,10},{10,18},{18,26},{... | collective-permute-start | bytes 393224 | tf_op jit(solution)/shard_map/ppermute | solution.py:17
  18.0 25.2 %copy-start.61 = (bf16[32,1,16,128]{3,0,2,1:T(8,128)(2,1)}, bf16[32,1,16,128]{3,0,2,1:T(8,128)(2,1)S(1)}, u32[]{:S(2)}) copy-start(bf16[32,1,16,128]{3,0,2,1:T(8,128)(2,1)S(1)} %collective-permute-done) | copy-start | bytes 393220
  18.2 27.4 %copy-start.59 = (bf16[32,1,16,128]{3,0,2,1:T(8,128)(2,1)}, bf16[32,1,16,128]{3,0,2,1:T(8,128)(2,1)S(1)}, u32[]{:S(2)}) copy-start(bf16[32,1,16,128]{3,0,2,1:T(8,128)(2,1)S(1)} %collective-permute-done.1) | copy-start | bytes 393220
  18.2 5.6 %collective-permute-start.2 = (bf16[32,4,1,128]{3,0,2,1:T(8,128)(2,1)S(1)}, bf16[32,4,1,128]{3,0,2,1:T(8,128)(2,1)S(1)}, u32[]{:S(2)}, u32[]{:S(2)}) collective-permute-start(bf16[32,4,1,128]{3,0,2,1:T(8,128)(2,1)S(1)} %get-tuple-element.136), channel_id=1, source_target_pairs={{0,4},{1,5},{2,6},{3,7},{8,12},{9,13},{10,14},{11,15},{16,20},{17,... | collective-permute-start | bytes 98312 | tf_op jit(solution)/shard_map/ppermute | solution.py:17
  21.8 5.8 %collective-permute-start.3 = (bf16[32,4,1,128]{3,0,2,1:T(8,128)(2,1)S(1)}, bf16[32,4,1,128]{3,0,2,1:T(8,128)(2,1)S(1)}, u32[]{:S(2)}, u32[]{:S(2)}) collective-permute-start(bf16[32,4,1,128]{3,0,2,1:T(8,128)(2,1)S(1)} %get-tuple-element.137), channel_id=1, source_target_pairs={{4,0},{5,1},{6,2},{7,3},{12,8},{13,9},{14,10},{15,11},{20,16},{21,... | collective-permute-start | bytes 98312 | tf_op jit(solution)/shard_map/ppermute | solution.py:19
  29.6 5.9 %collective-permute-start.5 = (bf16[32,4,18,1]{0,1,3,2:T(4,128)(2,1)S(1)}, bf16[32,4,18,1]{0,1,3,2:T(4,128)(2,1)}, u32[]{:S(2)}, u32[]{:S(2)}) collective-permute-start(bf16[32,4,18,1]{0,1,3,2:T(4,128)(2,1)S(1)} %copy.139), channel_id=1, source_target_pairs={{1,0},{2,1},{3,2},{5,4},{6,5},{7,6},{9,8},{10,9},{11,10},{13,12},{... | collective-permute-start | bytes 13832 | tf_op jit(solution)/shard_map/ppermute | solution.py:19
  30.9 4.1 %collective-permute-start.4 = (bf16[32,4,18,1]{0,1,3,2:T(4,128)(2,1)}, bf16[32,4,18,1]{0,1,3,2:T(4,128)(2,1)S(1)}, u32[]{:S(2)}, u32[]{:S(2)}) collective-permute-start(bf16[32,4,18,1]{0,1,3,2:T(4,128)(2,1)} %copy.137), channel_id=1, source_target_pairs={{0,1},{1,2},{2,3},{4,5},{5,6},{6,7},{8,9},{9,10},{10,11},{12,13},{... | collective-permute-start | bytes 13832 | tf_op jit(solution)/shard_map/ppermute | solution.py:17
  34.0 8.7 %copy-start.13 = (bf16[32,2,16,128]{3,0,2,1:T(8,128)(2,1)}, bf16[32,2,16,128]{3,0,2,1:T(8,128)(2,1)S(1)}, u32[]{:S(2)}) copy-start(bf16[32,2,16,128]{3,0,2,1:T(8,128)(2,1)S(1)} %get-tuple-element.134) | copy-start | bytes 786436
  34.0 9.5 %copy-start.15 = (bf16[32,2,16,128]{3,0,2,1:T(8,128)(2,1)}, bf16[32,2,16,128]{3,0,2,1:T(8,128)(2,1)S(1)}, u32[]{:S(2)}) copy-start(bf16[32,2,16,128]{3,0,2,1:T(8,128)(2,1)S(1)} %get-tuple-element.125) | copy-start | bytes 786436
  34.0 10.2 %copy-start.17 = (bf16[32,2,16,128]{3,0,2,1:T(8,128)(2,1)}, bf16[32,2,16,128]{3,0,2,1:T(8,128)(2,1)S(1)}, u32[]{:S(2)}) copy-start(bf16[32,2,16,128]{3,0,2,1:T(8,128)(2,1)S(1)} %get-tuple-element.135) | copy-start | bytes 786436
  34.0 10.9 %copy-start.23 = (bf16[32,2,16,128]{3,0,2,1:T(8,128)(2,1)}, bf16[32,2,16,128]{3,0,2,1:T(8,128)(2,1)S(1)}, u32[]{:S(2)}) copy-start(bf16[32,2,16,128]{3,0,2,1:T(8,128)(2,1)S(1)} %get-tuple-element.124) | copy-start | bytes 786436
  37.6 1.3 copy-start.95
  38.7 4.0 %copy-start.41 = (bf16[32,2,16,128]{3,0,2,1:T(8,128)(2,1)}, bf16[32,2,16,128]{3,0,2,1:T(8,128)(2,1)S(1)}, u32[]{:S(2)}) copy-start(bf16[32,2,16,128]{3,0,2,1:T(8,128)(2,1)S(1)} %get-tuple-element.98) | copy-start | bytes 786436
  38.7 4.0 %copy-start.43 = (bf16[32,2,16,128]{3,0,2,1:T(8,128)(2,1)}, bf16[32,2,16,128]{3,0,2,1:T(8,128)(2,1)S(1)}, u32[]{:S(2)}) copy-start(bf16[32,2,16,128]{3,0,2,1:T(8,128)(2,1)S(1)} %get-tuple-element.187) | copy-start | bytes 786436
  38.7 4.5 %copy-start.25 = (bf16[32,2,16,128]{3,0,2,1:T(8,128)(2,1)}, bf16[32,2,16,128]{3,0,2,1:T(8,128)(2,1)S(1)}, u32[]{:S(2)}) copy-start(bf16[32,2,16,128]{3,0,2,1:T(8,128)(2,1)S(1)} %get-tuple-element.97) | copy-start | bytes 786436
  38.7 4.5 %copy-start.27 = (bf16[32,2,16,128]{3,0,2,1:T(8,128)(2,1)}, bf16[32,2,16,128]{3,0,2,1:T(8,128)(2,1)S(1)}, u32[]{:S(2)}) copy-start(bf16[32,2,16,128]{3,0,2,1:T(8,128)(2,1)S(1)} %get-tuple-element.188) | copy-start | bytes 786436
  38.7 4.8 %copy-start.45 = (bf16[32,2,16,128]{3,0,2,1:T(8,128)(2,1)}, bf16[32,2,16,128]{3,0,2,1:T(8,128)(2,1)S(1)}, u32[]{:S(2)}) copy-start(bf16[32,2,16,128]{3,0,2,1:T(8,128)(2,1)S(1)} %get-tuple-element.96) | copy-start | bytes 786436
  38.7 4.8 %copy-start.47 = (bf16[32,2,16,128]{3,0,2,1:T(8,128)(2,1)}, bf16[32,2,16,128]{3,0,2,1:T(8,128)(2,1)S(1)}, u32[]{:S(2)}) copy-start(bf16[32,2,16,128]{3,0,2,1:T(8,128)(2,1)S(1)} %get-tuple-element.189) | copy-start | bytes 786436
  38.7 5.5 %copy-start.49 = (bf16[32,2,16,128]{3,0,2,1:T(8,128)(2,1)}, bf16[32,2,16,128]{3,0,2,1:T(8,128)(2,1)S(1)}, u32[]{:S(2)}) copy-start(bf16[32,2,16,128]{3,0,2,1:T(8,128)(2,1)S(1)} %get-tuple-element.95) | copy-start | bytes 786436
  38.7 5.5 %copy-start.51 = (bf16[32,2,16,128]{3,0,2,1:T(8,128)(2,1)}, bf16[32,2,16,128]{3,0,2,1:T(8,128)(2,1)S(1)}, u32[]{:S(2)}) copy-start(bf16[32,2,16,128]{3,0,2,1:T(8,128)(2,1)S(1)} %get-tuple-element.190) | copy-start | bytes 786436
  38.7 5.8 %copy-start.37 = (bf16[32,2,16,128]{3,0,2,1:T(8,128)(2,1)}, bf16[32,2,16,128]{3,0,2,1:T(8,128)(2,1)S(1)}, u32[]{:S(2)}) copy-start(bf16[32,2,16,128]{3,0,2,1:T(8,128)(2,1)S(1)} %get-tuple-element.94) | copy-start | bytes 786436
  38.8 5.8 %copy-start.39 = (bf16[32,2,16,128]{3,0,2,1:T(8,128)(2,1)}, bf16[32,2,16,128]{3,0,2,1:T(8,128)(2,1)S(1)}, u32[]{:S(2)}) copy-start(bf16[32,2,16,128]{3,0,2,1:T(8,128)(2,1)S(1)} %get-tuple-element.191) | copy-start | bytes 786436
  38.8 6.2 %copy-start.53 = (bf16[32,2,16,128]{3,0,2,1:T(8,128)(2,1)}, bf16[32,2,16,128]{3,0,2,1:T(8,128)(2,1)S(1)}, u32[]{:S(2)}) copy-start(bf16[32,2,16,128]{3,0,2,1:T(8,128)(2,1)S(1)} %get-tuple-element.93) | copy-start | bytes 786436
  38.8 6.2 %copy-start.55 = (bf16[32,2,16,128]{3,0,2,1:T(8,128)(2,1)}, bf16[32,2,16,128]{3,0,2,1:T(8,128)(2,1)S(1)}, u32[]{:S(2)}) copy-start(bf16[32,2,16,128]{3,0,2,1:T(8,128)(2,1)S(1)} %get-tuple-element.192) | copy-start | bytes 786436
  38.8 6.5 %copy-start.33 = (bf16[32,2,16,128]{3,0,2,1:T(8,128)(2,1)}, bf16[32,2,16,128]{3,0,2,1:T(8,128)(2,1)S(1)}, u32[]{:S(2)}) copy-start(bf16[32,2,16,128]{3,0,2,1:T(8,128)(2,1)S(1)} %get-tuple-element.92) | copy-start | bytes 786436
  38.8 6.5 %copy-start.35 = (bf16[32,2,16,128]{3,0,2,1:T(8,128)(2,1)}, bf16[32,2,16,128]{3,0,2,1:T(8,128)(2,1)S(1)}, u32[]{:S(2)}) copy-start(bf16[32,2,16,128]{3,0,2,1:T(8,128)(2,1)S(1)} %get-tuple-element.193) | copy-start | bytes 786436
  38.8 6.8 %copy-start.19 = (bf16[32,2,16,128]{3,0,2,1:T(8,128)(2,1)}, bf16[32,2,16,128]{3,0,2,1:T(8,128)(2,1)S(1)}, u32[]{:S(2)}) copy-start(bf16[32,2,16,128]{3,0,2,1:T(8,128)(2,1)S(1)} %get-tuple-element.91) | copy-start | bytes 786436
  38.8 6.8 %copy-start.21 = (bf16[32,2,16,128]{3,0,2,1:T(8,128)(2,1)}, bf16[32,2,16,128]{3,0,2,1:T(8,128)(2,1)S(1)}, u32[]{:S(2)}) copy-start(bf16[32,2,16,128]{3,0,2,1:T(8,128)(2,1)S(1)} %get-tuple-element.194) | copy-start | bytes 786436
  38.8 7.1 %copy-start.29 = (bf16[32,2,16,128]{3,0,2,1:T(8,128)(2,1)}, bf16[32,2,16,128]{3,0,2,1:T(8,128)(2,1)S(1)}, u32[]{:S(2)}) copy-start(bf16[32,2,16,128]{3,0,2,1:T(8,128)(2,1)S(1)} %get-tuple-element.90) | copy-start | bytes 786436
  38.8 7.1 %copy-start.31 = (bf16[32,2,16,128]{3,0,2,1:T(8,128)(2,1)}, bf16[32,2,16,128]{3,0,2,1:T(8,128)(2,1)S(1)}, u32[]{:S(2)}) copy-start(bf16[32,2,16,128]{3,0,2,1:T(8,128)(2,1)S(1)} %get-tuple-element.195) | copy-start | bytes 786436
  42.4 3.5 %copy-start.10 = (f32[32,2,16,128]{3,0,2,1:T(8,128)}, f32[32,2,16,128]{3,0,2,1:T(8,128)S(1)}, u32[]{:S(2)}) copy-start(f32[32,2,16,128]{3,0,2,1:T(8,128)S(1)} %fusion.5) | copy-start | bytes 1572868
  45.9 6.2 %copy-start.5 = (bf16[3,3,3,32,32]{4,3,2,1,0:T(8,128)(2,1)S(1)}, bf16[3,3,3,32,32]{4,3,2,1,0:T(8,128)(2,1)}, u32[]{:S(2)}) copy-start(bf16[3,3,3,32,32]{4,3,2,1,0:T(8,128)(2,1)} %param.7) | copy-start | bytes 165892
  46.5 10.8 %collective-permute-start.6 = (bf16[2,32,1,16,128]{4,1,3,2,0:T(8,128)(2,1)S(1)}, bf16[2,32,1,16,128]{4,1,3,2,0:T(8,128)(2,1)S(1)}, u32[]{:S(2)}, u32[]{:S(2)}) collective-permute-start(bf16[2,32,1,16,128]{4,1,3,2,0:T(8,128)(2,1)S(1)} %get-tuple-element.132), channel_id=1, source_target_pairs={{0,8},{8,16},{16,24},{1,9},{9,17},{17,25},{2,10},{10,18},{18,26},{... | collective-permute-start | bytes 786440 | tf_op jit(solution)/shard_map/ppermute | solution.py:17
  50.8 11.0 %collective-permute-start.7 = (bf16[2,32,1,16,128]{4,1,3,2,0:T(8,128)(2,1)S(1)}, bf16[2,32,1,16,128]{4,1,3,2,0:T(8,128)(2,1)S(1)}, u32[]{:S(2)}, u32[]{:S(2)}) collective-permute-start(bf16[2,32,1,16,128]{4,1,3,2,0:T(8,128)(2,1)S(1)} %get-tuple-element.133), channel_id=1, source_target_pairs={{8,0},{16,8},{24,16},{9,1},{17,9},{25,17},{10,2},{18,10},{26,18},{... | collective-permute-start | bytes 786440 | tf_op jit(solution)/shard_map/ppermute | solution.py:19
  57.3 12.4 %copy-start = (bf16[2,32,1,16,128]{4,1,3,2,0:T(8,128)(2,1)}, bf16[2,32,1,16,128]{4,1,3,2,0:T(8,128)(2,1)S(1)}, u32[]{:S(2)}) copy-start(bf16[2,32,1,16,128]{4,1,3,2,0:T(8,128)(2,1)S(1)} %collective-permute-done.6) | copy-start | bytes 786436
  61.9 7.8 %copy-start.1 = (bf16[2,32,1,16,128]{4,1,3,2,0:T(8,128)(2,1)}, bf16[2,32,1,16,128]{4,1,3,2,0:T(8,128)(2,1)S(1)}, u32[]{:S(2)}) copy-start(bf16[2,32,1,16,128]{4,1,3,2,0:T(8,128)(2,1)S(1)} %collective-permute-done.7) | copy-start | bytes 786436
  61.9 3.7 %collective-permute-start.8 = (bf16[2,32,4,1,128]{4,1,3,2,0:T(8,128)(2,1)S(1)}, bf16[2,32,4,1,128]{4,1,3,2,0:T(8,128)(2,1)S(1)}, u32[]{:S(2)}, u32[]{:S(2)}) collective-permute-start(bf16[2,32,4,1,128]{4,1,3,2,0:T(8,128)(2,1)S(1)} %get-tuple-element.108), channel_id=1, source_target_pairs={{0,4},{1,5},{2,6},{3,7},{8,12},{9,13},{10,14},{11,15},{16,20},{17,... | collective-permute-start | bytes 196616 | tf_op jit(solution)/shard_map/ppermute | solution.py:17
  63.5 6.2 %collective-permute-start.9 = (bf16[2,32,4,1,128]{4,1,3,2,0:T(8,128)(2,1)S(1)}, bf16[2,32,4,1,128]{4,1,3,2,0:T(8,128)(2,1)S(1)}, u32[]{:S(2)}, u32[]{:S(2)}) collective-permute-start(bf16[2,32,4,1,128]{4,1,3,2,0:T(8,128)(2,1)S(1)} %get-tuple-element.109), channel_id=1, source_target_pairs={{4,0},{5,1},{6,2},{7,3},{12,8},{13,9},{14,10},{15,11},{20,16},{21,... | collective-permute-start | bytes 196616 | tf_op jit(solution)/shard_map/ppermute | solution.py:19
  72.6 7.1 %copy-start.72 = (bf16[1,1,3,32,32]{3,4,2,1,0:T(8,128)(2,1)S(1)}, bf16[1,1,3,32,32]{3,4,2,1,0:T(8,128)(2,1)}, u32[]{:S(2)}) copy-start(bf16[1,1,3,32,32]{3,4,2,1,0:T(8,128)(2,1)} %get-tuple-element.142) | copy-start | bytes 18436
  72.6 7.2 %copy-start.71 = (bf16[1,1,3,32,32]{3,4,2,1,0:T(8,128)(2,1)S(1)}, bf16[1,1,3,32,32]{3,4,2,1,0:T(8,128)(2,1)}, u32[]{:S(2)}) copy-start(bf16[1,1,3,32,32]{3,4,2,1,0:T(8,128)(2,1)} %get-tuple-element.143) | copy-start | bytes 18436
  72.6 7.3 %copy-start.70 = (bf16[1,1,3,32,32]{3,4,2,1,0:T(8,128)(2,1)S(1)}, bf16[1,1,3,32,32]{3,4,2,1,0:T(8,128)(2,1)}, u32[]{:S(2)}) copy-start(bf16[1,1,3,32,32]{3,4,2,1,0:T(8,128)(2,1)} %get-tuple-element.144) | copy-start | bytes 18436
  72.6 8.0 %copy-start.69 = (bf16[1,1,3,32,32]{3,4,2,1,0:T(8,128)(2,1)S(1)}, bf16[1,1,3,32,32]{3,4,2,1,0:T(8,128)(2,1)}, u32[]{:S(2)}) copy-start(bf16[1,1,3,32,32]{3,4,2,1,0:T(8,128)(2,1)} %get-tuple-element.145) | copy-start | bytes 18436
  72.6 8.7 %copy-start.68 = (bf16[1,1,3,32,32]{3,4,2,1,0:T(8,128)(2,1)S(1)}, bf16[1,1,3,32,32]{3,4,2,1,0:T(8,128)(2,1)}, u32[]{:S(2)}) copy-start(bf16[1,1,3,32,32]{3,4,2,1,0:T(8,128)(2,1)} %get-tuple-element.146) | copy-start | bytes 18436
  72.6 9.4 %copy-start.67 = (bf16[1,1,3,32,32]{3,4,2,1,0:T(8,128)(2,1)S(1)}, bf16[1,1,3,32,32]{3,4,2,1,0:T(8,128)(2,1)}, u32[]{:S(2)}) copy-start(bf16[1,1,3,32,32]{3,4,2,1,0:T(8,128)(2,1)} %get-tuple-element.147) | copy-start | bytes 18436
  72.6 10.1 %copy-start.66 = (bf16[1,1,3,32,32]{3,4,2,1,0:T(8,128)(2,1)S(1)}, bf16[1,1,3,32,32]{3,4,2,1,0:T(8,128)(2,1)}, u32[]{:S(2)}) copy-start(bf16[1,1,3,32,32]{3,4,2,1,0:T(8,128)(2,1)} %get-tuple-element.148) | copy-start | bytes 18436
  72.7 10.8 %copy-start.65 = (bf16[1,1,3,32,32]{3,4,2,1,0:T(8,128)(2,1)S(1)}, bf16[1,1,3,32,32]{3,4,2,1,0:T(8,128)(2,1)}, u32[]{:S(2)}) copy-start(bf16[1,1,3,32,32]{3,4,2,1,0:T(8,128)(2,1)} %get-tuple-element.149) | copy-start | bytes 18436
  72.7 11.5 %copy-start.64 = (bf16[1,1,3,32,32]{3,4,2,1,0:T(8,128)(2,1)S(1)}, bf16[1,1,3,32,32]{3,4,2,1,0:T(8,128)(2,1)}, u32[]{:S(2)}) copy-start(bf16[1,1,3,32,32]{3,4,2,1,0:T(8,128)(2,1)} %get-tuple-element.150) | copy-start | bytes 18436
  73.6 12.3 %collective-permute-start.11 = (bf16[2,32,4,18,1]{1,2,4,3,0:T(4,128)(2,1)S(1)}, bf16[2,32,4,18,1]{1,2,4,3,0:T(4,128)(2,1)}, u32[]{:S(2)}, u32[]{:S(2)}) collective-permute-start(bf16[2,32,4,18,1]{1,2,4,3,0:T(4,128)(2,1)S(1)} %copy.163), channel_id=1, source_target_pairs={{1,0},{2,1},{3,2},{5,4},{6,5},{7,6},{9,8},{10,9},{11,10},{13,12},{... | collective-permute-start | bytes 27656 | tf_op jit(solution)/shard_map/ppermute | solution.py:19
  74.9 10.0 %collective-permute-start.10 = (bf16[2,32,4,18,1]{1,2,4,3,0:T(4,128)(2,1)}, bf16[2,32,4,18,1]{1,2,4,3,0:T(4,128)(2,1)S(1)}, u32[]{:S(2)}, u32[]{:S(2)}) collective-permute-start(bf16[2,32,4,18,1]{1,2,4,3,0:T(4,128)(2,1)} %copy.162), channel_id=1, source_target_pairs={{0,1},{1,2},{2,3},{4,5},{5,6},{6,7},{8,9},{9,10},{10,11},{12,13},{... | collective-permute-start | bytes 27656 | tf_op jit(solution)/shard_map/ppermute | solution.py:17
  93.9 1.2 copy-start.89
  106.1 7.3 %collective-permute-start.12 = (bf16[32,1,16,128]{3,0,2,1:T(8,128)(2,1)S(1)}, bf16[32,1,16,128]{3,0,2,1:T(8,128)(2,1)S(1)}, u32[]{:S(2)}, u32[]{:S(2)}) collective-permute-start(bf16[32,1,16,128]{3,0,2,1:T(8,128)(2,1)S(1)} %get-tuple-element.138), channel_id=1, source_target_pairs={{0,8},{8,16},{16,24},{1,9},{9,17},{17,25},{2,10},{10,18},{18,26},{... | collective-permute-start | bytes 393224 | tf_op jit(solution)/shard_map/ppermute | solution.py:17
  109.6 7.9 %collective-permute-start.13 = (bf16[32,1,16,128]{3,0,2,1:T(8,128)(2,1)S(1)}, bf16[32,1,16,128]{3,0,2,1:T(8,128)(2,1)S(1)}, u32[]{:S(2)}, u32[]{:S(2)}) collective-permute-start(bf16[32,1,16,128]{3,0,2,1:T(8,128)(2,1)S(1)} %get-tuple-element.139), channel_id=1, source_target_pairs={{8,0},{16,8},{24,16},{9,1},{17,9},{25,17},{10,2},{18,10},{26,18},{... | collective-permute-start | bytes 393224 | tf_op jit(solution)/shard_map/ppermute | solution.py:19
  117.5 4.1 %collective-permute-start.14 = (bf16[32,4,1,128]{3,0,2,1:T(8,128)(2,1)S(1)}, bf16[32,4,1,128]{3,0,2,1:T(8,128)(2,1)S(1)}, u32[]{:S(2)}, u32[]{:S(2)}) collective-permute-start(bf16[32,4,1,128]{3,0,2,1:T(8,128)(2,1)S(1)} %get-tuple-element.130), channel_id=1, source_target_pairs={{0,4},{1,5},{2,6},{3,7},{8,12},{9,13},{10,14},{11,15},{16,20},{17,... | collective-permute-start | bytes 98312 | tf_op jit(solution)/shard_map/ppermute | solution.py:17
  119.1 5.8 %collective-permute-start.15 = (bf16[32,4,1,128]{3,0,2,1:T(8,128)(2,1)S(1)}, bf16[32,4,1,128]{3,0,2,1:T(8,128)(2,1)S(1)}, u32[]{:S(2)}, u32[]{:S(2)}) collective-permute-start(bf16[32,4,1,128]{3,0,2,1:T(8,128)(2,1)S(1)} %get-tuple-element.131), channel_id=1, source_target_pairs={{4,0},{5,1},{6,2},{7,3},{12,8},{13,9},{14,10},{15,11},{20,16},{21,... | collective-permute-start | bytes 98312 | tf_op jit(solution)/shard_map/ppermute | solution.py:19
  126.3 6.0 %collective-permute-start.17 = (bf16[32,4,18,1]{0,1,3,2:T(4,128)(2,1)S(1)}, bf16[32,4,18,1]{0,1,3,2:T(4,128)(2,1)S(1)}, u32[]{:S(2)}, u32[]{:S(2)}) collective-permute-start(bf16[32,4,18,1]{0,1,3,2:T(4,128)(2,1)S(1)} %copy.186), channel_id=1, source_target_pairs={{1,0},{2,1},{3,2},{5,4},{6,5},{7,6},{9,8},{10,9},{11,10},{13,12},{... | collective-permute-start | bytes 13832 | tf_op jit(solution)/shard_map/ppermute | solution.py:19
  127.6 4.2 %collective-permute-start.16 = (bf16[32,4,18,1]{0,1,3,2:T(4,128)(2,1)S(1)}, bf16[32,4,18,1]{0,1,3,2:T(4,128)(2,1)S(1)}, u32[]{:S(2)}, u32[]{:S(2)}) collective-permute-start(bf16[32,4,18,1]{0,1,3,2:T(4,128)(2,1)S(1)} %copy.184), channel_id=1, source_target_pairs={{0,1},{1,2},{2,3},{4,5},{5,6},{6,7},{8,9},{9,10},{10,11},{12,13},{... | collective-permute-start | bytes 13832 | tf_op jit(solution)/shard_map/ppermute | solution.py:17
  150.2 1.1 copy-start.7
  150.2 1.3 copy-start.8
  282.5 2.4 copy-start.9
  (62 other events, 54.3 us)
Sparse Core Ops, SparseCore 0:
  151.4 130.9 all-reduce.2
where the time goes:
time: 295 us; the launch traced here: 293 us
  waiting for transfers between devices  158 us (54%)
  local copies, waits for them, and re-layouts  47.3 us (16%)
  starting transfers between devices  41.4 us (14%)
  matrix products  19.3 us (7%)
  between operations  15.7 us (5%)
  other arithmetic  10.9 us (4%)
    psum x1, waiting for transfers between devices, body(): lax.psum((local_first, local_second), ('gx', 'gy', 'gz'))  130 us
    ppermute x9, starting transfers between devices, padded_2(): lax.ppermute(tail, axis, [(i, (i + 1) % count) for i in range(ends)])  29.5 us
    ppermute x9, waiting for transfers between devices, padded_2(): lax.ppermute(head, axis, [((i + 1) % count, i) for i in range(ends)])  19.9 us
    unnamed x222, local copies, waits for them, and re-layouts  16.6 us
    dot_general x45, matrix products, stencil(): jnp.einsum('kxyz,ko->oxyz', stacked, matrix, preferred_element_type=jnp.f...  12.7 us
    ppermute x9, starting transfers between devices, padded_2(): lax.ppermute(head, axis, [((i + 1) % count, i) for i in range(ends)])  11.8 us
    ppermute x9, waiting for transfers between devices, padded_2(): lax.ppermute(tail, axis, [(i, (i + 1) % count) for i in range(ends)])  8.55 us
    dot_general x18, matrix products, correlate(): jnp.einsum('kxyz,oxyz->ko', stacked, target, preferred_element_type=jnp.f...  6.62 us
  transfers between devices with their start and end apart: 19, of which 10 were waited for; matrix products, arithmetic and copies ran while one was open for 6% of the time, Pallas kernels for 0%

commit v1 on v0

v1 whole, which is shorter than its diff:
```python
import functools
import itertools
import math

import jax
import jax.numpy as jnp
from jax import lax
from jax.experimental import pallas as pl
from jax.experimental.pallas import tpu as pltpu
from jax.sharding import PartitionSpec as P

MESH = pl.DeviceIdType.MESH
AXES = ("gx", "gy", "gz")
STEPS = [d for d in itertools.product((-1, 0, 1), repeat=3) if d != (0, 0, 0)]
STEPS.sort(key=lambda d: (d[2] != 0, d[0] == 0, abs(d[0]) + abs(d[1])))
NT = (((1,), (1,)), ((), ()))


def gelu_pair(pre):
    inner = 0.7978845608 * (pre + 0.044715 * pre * pre * pre)
    hyper = jnp.tanh(inner)
    hidden = 0.5 * pre * (1.0 + hyper)
    slope = 0.5 * (1.0 + hyper) + 0.5 * pre * (1.0 - hyper * hyper) * 0.7978845608 * (
        1.0 + 0.134145 * pre * pre
    )
    return hidden, slope


def code(step):
    return (step[0] + 1) * 9 + (step[1] + 1) * 3 + step[2] + 1


def kernel(
    sizes,
    volume,
    w1,
    w2,
    w3,
    jv_out,
    gv1,
    gv2,
    *scratch,
):
    (rv, rp, rj, zv, zp, zj, ev, ep, ej, sv, sp, slope_ref, back_ref, acc, pack, land, part, full,
     hsend, hrecv, asend, arecv, bsend, brecv) = scratch
    depth, height, chan, width = volume.shape
    me = tuple(lax.axis_index(a) for a in AXES)
    total = sizes[0] * sizes[1] * sizes[2]
    line = (me[0] * sizes[1] + me[1]) * sizes[2] + me[2]

    def place(index):
        return (
            index // (sizes[1] * sizes[2]),
            index // sizes[2] % sizes[1],
            index % sizes[2],
        )

    barrier = pltpu.get_barrier_semaphore()

    @pl.loop(1, total)
    def _(i):
        pl.semaphore_signal(
            barrier, inc=1, device_id=place(lax.rem(line + i, total)), device_id_type=MESH
        )

    def there(step):
        ok = None
        for pos, size, delta in zip(me, sizes, step):
            if delta == -1:
                term = pos > 0
            elif delta == 1:
                term = pos < size - 1
            else:
                continue
            ok = term if ok is None else jnp.logical_and(ok, term)
        return ok

    def source(delta, extent):
        return {-1: pl.ds(1, 1), 1: pl.ds(extent, 1), 0: pl.ds(1, extent)}[delta]

    def target(delta, extent):
        return {-1: pl.ds(extent + 1, 1), 1: pl.ds(0, 1), 0: pl.ds(1, extent)}[delta]

    def landing(step, rows, zbuf):
        if step[2] == 0:
            return rows.at[target(step[0], depth), target(step[1], height)]
        return zbuf.at[0 if step[2] == 1 else 1, 1 - step[0], 1 - step[1]]

    def message(step, rows, zbuf, edge, slot):
        if step[2] == 0:
            src = rows.at[source(step[0], depth), source(step[1], height)]
        else:
            src = edge
        return pltpu.make_async_remote_copy(
            src_ref=src,
            dst_ref=landing(step, rows, zbuf),
            send_sem=hsend.at[slot, code(step)],
            recv_sem=hrecv.at[slot, code(step)],
            device_id=tuple(p + d for p, d in zip(me, step)),
            device_id_type=MESH,
        )

    def send(rows, zbuf, edge, slot, cross):
        for step in STEPS:
            if (step[2] != 0) == cross:

                @pl.when(there(step))
                def _():
                    message(step, rows, zbuf, edge, slot).start()

    def clear(rows, zbuf):
        for step in STEPS:
            back = tuple(-d for d in step)

            @pl.when(jnp.logical_not(there(back)))
            def _():
                ref = landing(step, rows, zbuf)
                ref[...] = jnp.zeros(ref.shape, ref.dtype)

    def receive(rows, zbuf, edge, slot):
        for step in STEPS:
            back = tuple(-d for d in step)

            @pl.when(there(back))
            def _():
                message(step, rows, zbuf, edge, slot).wait_recv()

    def sent(rows, zbuf, edge, slot):
        for step in STEPS:

            @pl.when(there(step))
            def _():
                message(step, rows, zbuf, edge, slot).wait_send()

    def edges(rows, edge):
        count = rows.shape[2]
        lane = lax.broadcasted_iota(jnp.int32, (count, width), 1)
        cells = depth * height
        built = jnp.zeros((count, width), jnp.float32)
        for x in range(depth):

            def step(y, built, x=x):
                row = rows[x + 1, y + 1].astype(jnp.float32)
                at = x * height + y
                built = jnp.where(lane == at, pltpu.roll(row, at, 1), built)
                return jnp.where(lane == cells + at, pltpu.roll(row, cells + at + 1, 1), built)

            built = lax.fori_loop(0, height, step, built, unroll=4)
        edge[...] = built.astype(edge.dtype)

    def spread(rows, zbuf, out):
        count = rows.shape[2]
        groups = count // chan
        lane = lax.broadcasted_iota(jnp.int32, (count, width), 1)
        cells = depth * height

        def one(xp, yp, dy, y):
            dx = 0 if xp == 0 else (2 if xp == depth + 1 else 1)
            at = (xp - 1) % depth * height + y
            row = rows[xp, yp]
            wide = row.astype(jnp.float32)
            left = zbuf[0, dx, dy].astype(jnp.float32)
            right = zbuf[1, dx, dy].astype(jnp.float32)
            low = jnp.where(
                lane == 0,
                pltpu.roll(left, width - cells - at, 1),
                pltpu.roll(wide, 1, 1),
            ).astype(row.dtype)
            high = jnp.where(
                lane == width - 1,
                pltpu.roll(right, width - 1 - at, 1),
                pltpu.roll(wide, width - 1, 1),
            ).astype(row.dtype)
            for g in range(groups):
                part_of = slice(g * chan, (g + 1) * chan)
                base = g * 3 * chan
                out[xp, yp, base : base + chan] = low[part_of]
                out[xp, yp, base + chan : base + 2 * chan] = row[part_of]
                out[xp, yp, base + 2 * chan : base + 3 * chan] = high[part_of]

        for xp in range(depth + 2):
            one(xp, 0, 0, height - 1)
            one(xp, height + 1, 2, 0)

            @pl.loop(0, height, unroll=2)
            def _(y, xp=xp):
                one(xp, y + 1, 1, y)

    def window(ref, x, y, span):
        return ref[pl.ds(x, span), pl.ds(y, 3)].reshape(span * 3 * ref.shape[2], width)

    def convolve(weights, ref, finish):
        for x in range(depth):

            @pl.loop(0, height // 2)
            def _(j, x=x):
                y = 2 * j
                rhs = jnp.concatenate([window(ref, x, y, 3), window(ref, x, y + 1, 3)], axis=1)
                out = jnp.dot(weights[...], rhs, preferred_element_type=jnp.float32)
                finish(x, y, out[:, :width])
                finish(x, y + 1, out[:, width:])

    def correlate(ref, rows, offset):
        acc[...] = jnp.zeros_like(acc)
        for x in range(depth):

            @pl.loop(0, height // 4)
            def _(j, x=x):
                y = 4 * j
                rhs = jnp.concatenate(
                    [rows[x + offset, y + i + offset] for i in range(4)], axis=1
                )
                for kx in range(3):
                    lhs = jnp.concatenate(
                        [
                            ref[x + kx, pl.ds(y + i, 3), : 3 * chan].reshape(9 * chan, width)
                            for i in range(4)
                        ],
                        axis=1,
                    )
                    acc[kx] += lax.dot_general(lhs, rhs, NT, preferred_element_type=jnp.float32)

    tiles = pack.shape[1]

    def owner(t):
        return t * total // tiles

    span = 8 * tiles
    lanes = width // chan

    def scatter(slot):
        for j in range(lanes):
            flat = acc[...].reshape(27 * chan, chan)
            pack[slot, :, :, j * chan : (j + 1) * chan] = flat[
                j * span : (j + 1) * span
            ].reshape(tiles, 8, chan)
        for t in range(tiles):
            at = owner(t)

            @pl.when(line != at)
            def _():
                pltpu.make_async_remote_copy(
                    src_ref=pack.at[slot, t],
                    dst_ref=land.at[slot, lax.rem(line - at + total, total) - 1],
                    send_sem=asend.at[slot],
                    recv_sem=arecv.at[slot],
                    device_id=place(at),
                    device_id_type=MESH,
                ).start()

    def gather(slot):
        for t in range(tiles):

            @pl.when(line == owner(t))
            def _():
                pltpu.make_async_copy(
                    land.at[slot], land.at[slot], arecv.at[slot]
                ).wait()
                summed = pack[slot, t] + jnp.sum(land[slot], axis=0)
                part[slot] = summed
                full[slot, t] = summed

                @pl.loop(1, total)
                def _(i):
                    pltpu.make_async_remote_copy(
                        src_ref=part.at[slot],
                        dst_ref=full.at[slot, t],
                        send_sem=bsend.at[slot],
                        recv_sem=brecv.at[slot],
                        device_id=place(lax.rem(line + i, total)),
                        device_id_type=MESH,
                    ).start()

    def owning():
        held = line == owner(0)
        for t in range(1, tiles):
            held = jnp.logical_or(held, line == owner(t))
        return held

    def drain(slot, out):
        held = owning()
        for flag, count in ((held, tiles - 1), (jnp.logical_not(held), tiles)):

            @pl.when(flag)
            def _():
                some = full.at[slot, pl.ds(0, count)]
                pltpu.make_async_copy(some, some, brecv.at[slot]).wait()
                mine = pack.at[slot, pl.ds(0, count)]
                pltpu.make_async_copy(mine, mine, asend.at[slot]).wait()

        @pl.when(held)
        def _():
            pltpu.make_async_copy(land.at[slot], land.at[slot], bsend.at[slot]).wait()

        whole = full[slot].reshape(span, width)
        for j in range(lanes):
            out[j * span : (j + 1) * span] = whole[:, j * chan : (j + 1) * chan]

    inner = (slice(1, depth + 1), slice(1, height + 1))
    rv[inner] = volume[...]
    edges(rv, ev)
    for rows, zbuf in ((rv, zv), (rp, zp), (rj, zj)):
        clear(rows, zbuf)
    pl.semaphore_wait(barrier, total - 1)

    send(rv, zv, ev, 0, False)
    send(rv, zv, ev, 0, True)
    receive(rv, zv, ev, 0)
    spread(rv, zv, sv)

    def first(x, y, out):
        hidden, slope = gelu_pair(out[:chan])
        slope_ref[x, y] = slope
        rp[x + 1, y + 1, :chan] = hidden.astype(jnp.bfloat16)
        rp[x + 1, y + 1, chan:] = (slope * out[chan:]).astype(jnp.bfloat16)

    convolve(w1, sv, first)
    send(rp, zp, ep, 1, False)
    edges(rp, ep)
    send(rp, zp, ep, 1, True)
    receive(rp, zp, ep, 1)
    spread(rp, zp, sp)

    def second(x, y, out):
        rj[x + 1, y + 1] = out.astype(jnp.bfloat16)

    convolve(w2, sp, second)
    send(rj, zj, ej, 2, False)
    edges(rj, ej)
    send(rj, zj, ej, 2, True)
    jv_out[...] = rj[inner]
    correlate(sp, rj, 1)
    scatter(0)
    receive(rj, zj, ej, 2)
    sj = sp.at[:, :, : 3 * chan]
    spread(rj, zj, sj)

    def third(x, y, out):
        back_ref[x, y] = (slope_ref[x, y] * out).astype(jnp.bfloat16)

    convolve(w3, sj, third)
    gather(0)
    correlate(sv, back_ref, 0)
    scatter(1)
    gather(1)
    drain(0, gv2)
    drain(1, gv1)
    sent(rv, zv, ev, 0)
    sent(rp, zp, ep, 1)
    sent(rj, zj, ej, 2)


def body(volume, w_first, w_second, v_first, v_second):
    chan, depth, height, width = volume.shape
    sizes = tuple(lax.axis_size(a) for a in AXES)
    total = sizes[0] * sizes[1] * sizes[2]
    filt = 27 * chan
    tiles = filt * chan // (8 * width)
    w1 = jnp.concatenate([w_first, v_first], axis=-1).reshape(filt, 2 * chan).T
    w2 = jnp.stack([v_second, w_second], axis=2).reshape(2 * filt, chan).T
    w3 = jnp.transpose(jnp.flip(w_second, (0, 1, 2)), (3, 0, 1, 2, 4)).reshape(chan, filt)
    cells = jnp.transpose(volume, (1, 2, 0, 3))
    bf, f32 = jnp.bfloat16, jnp.float32
    pads = (depth + 2, height + 2)
    vmem = pl.BlockSpec(memory_space=pltpu.VMEM)
    jv, corr1, corr2 = pl.pallas_call(
        functools.partial(kernel, sizes),
        out_shape=(
            jax.ShapeDtypeStruct((depth, height, chan, width), bf),
            jax.ShapeDtypeStruct((filt, chan), f32),
            jax.ShapeDtypeStruct((filt, chan), f32),
        ),
        in_specs=[vmem] * 4,
        out_specs=(vmem,) * 3,
        scratch_shapes=[
            pltpu.VMEM(pads + (chan, width), bf),
            pltpu.VMEM(pads + (2 * chan, width), bf),
            pltpu.VMEM(pads + (chan, width), bf),
            pltpu.VMEM((2, 3, 3, chan, width), bf),
            pltpu.VMEM((2, 3, 3, 2 * chan, width), bf),
            pltpu.VMEM((2, 3, 3, chan, width), bf),
            pltpu.VMEM((chan, width), bf),
            pltpu.VMEM((2 * chan, width), bf),
            pltpu.VMEM((chan, width), bf),
            pltpu.VMEM(pads + (3 * chan, width), bf),
            pltpu.VMEM(pads + (6 * chan, width), bf),
            pltpu.VMEM((depth, height, chan, width), f32),
            pltpu.VMEM((depth, height, chan, width), bf),
            pltpu.VMEM((3, 9 * chan, chan), f32),
            pltpu.VMEM((2, tiles, 8, width), f32),
            pltpu.VMEM((2, total - 1, 8, width), f32),
            pltpu.VMEM((2, 8, width), f32),
            pltpu.VMEM((2, tiles, 8, width), f32),
            pltpu.SemaphoreType.DMA((3, 27)),
            pltpu.SemaphoreType.DMA((3, 27)),
            pltpu.SemaphoreType.DMA((2,)),
            pltpu.SemaphoreType.DMA((2,)),
            pltpu.SemaphoreType.DMA((2,)),
            pltpu.SemaphoreType.DMA((2,)),
        ],
        compiler_params=pltpu.CompilerParams(
            collective_id=0, has_side_effects=True, vmem_limit_bytes=48 * 1024 * 1024
        ),
    )(cells, w1, w2, w3)
    count = float(depth * height * width * total)
    factor = math.sqrt(27.0 * chan)
    gv_first = factor * (corr1.reshape(v_first.shape) / count + 0.1 * v_first.astype(f32))
    gv_second = factor * (corr2.reshape(v_second.shape) / count + 0.1 * v_second.astype(f32))
    return jnp.transpose(jv, (2, 0, 1, 3)), gv_first, gv_second


def solution(mesh):
    in_specs = (P(None, "gx", "gy", "gz"), P(), P(), P(), P())
    out_specs = (P(None, "gx", "gy", "gz"), P(), P())
    return jax.shard_map(body, mesh=mesh, in_specs=in_specs, out_specs=out_specs, check_vma=False)
```

time: 295 us -> 74.3 us (0.25)
  waiting for transfers between devices: 158 us -> 0 us
  Pallas kernels: 0 us -> 65.6 us
  local copies, waits for them, and re-layouts: 47.3 us -> 4.74 us
  starting transfers between devices: 41.4 us -> 0 us
  matrix products: 19.3 us -> 0 us
  between operations: 15.7 us -> 0.71 us
  other arithmetic: 10.9 us -> 3.02 us
    psum x1 -> x0, waiting for transfers between devices: 130 us -> none  [body(): lax.psum((local_first, local_second), ('gx', 'gy', 'gz'))]
    pallas_call x0 -> x1, Pallas kernels: none -> 65.6 us  [body(): pl.pallas_call(functools.partial(kernel, sizes), out_shape=(jax.ShapeDtyp...]
    ppermute x18 -> x0, starting transfers between devices: 41.3 us -> none  [the longest x9 29.5 us: padded_2(): lax.ppermute(tail, axis, [(i, (i + 1) % count) for i in range(ends)])]
    ppermute x18 -> x0, waiting for transfers between devices: 28.5 us -> none  [the longest x9 19.9 us: padded_2(): lax.ppermute(head, axis, [((i + 1) % count, i) for i in range(ends)])]
    dot_general x63 -> x0, matrix products: 19.3 us -> none  [the longest x45 12.7 us: stencil(): jnp.einsum('kxyz,ko->oxyz', stacked, matrix, preferred_element_type=jnp.f...]
    slice x35 -> x0, local copies, waits for them, and re-layouts: 18.1 us -> none  [the longest x9 6.55 us: stencil(): padded[:, shift_x:shift_x + depth, shift_y:shift_y + height, shift_z:shif...]
    unnamed x222 -> x10, local copies, waits for them, and re-layouts: 16.6 us -> 3.37 us
    another operation x27 -> x1, local copies, waits for them, and re-layouts: 6.67 us -> 0.58 us  [body(): w2 = jnp.stack([v_second, w_second], axis=2).reshape(2 * filt, chan).T]
  transfers between devices with their start and end apart: 19 -> 0, of which waited for: 10 -> 0; matrix products, arithmetic and copies ran while one was open for 6% -> 0% of each run, Pallas kernels for 0% -> 0%
where the time goes in v1:
time: 74.3 us; the launch traced here: 74.1 us
  Pallas kernels  65.6 us (88%)
  local copies, waits for them, and re-layouts  4.74 us (6%)
  other arithmetic  3.02 us (4%)
    pallas_call x1, Pallas kernels, body(): pl.pallas_call(functools.partial(kernel, sizes), out_shape=(jax.ShapeDtyp...  65.6 us
    unnamed x10, local copies, waits for them, and re-layouts  3.37 us

profile of v1, /device:TPU:0, one launch (start us, length us, event | category | flops | bytes accessed | tf_op | source)
XLA Modules:
  0.0 74.1 jit_solution(1732969602228496459)
XLA Ops:
  0.6 1.2 %pad_maximum_fusion.1 = bf16[3,3,3,32,64]{4,3,2,1,0:T(8,128)(2,1)S(1)} fusion(bf16[3,3,3,32,32]{4,3,2,1,0:T(8,128)(2,1)} %param.8, bf16[3,3,3,32,32]{4,3,2,1,0:T(8,128)(2,1)} %param.6), kind=kLoop, calls=%fused_computation.4 | loop fusion | flops 221184 | bytes 221184 | tf_op jit(solution)/shard_map/concatenate | solution.py:359
  1.8 0.0 copy-start
  1.8 0.1 copy.14
  2.0 0.8 %copy-done = bf16[3,3,3,32,32]{4,3,2,1,0:T(8,128)(2,1)S(1)} copy-done((bf16[3,3,3,32,32]{4,3,2,1,0:T(8,128)(2,1)S(1)}, bf16[3,3,3,32,32]{4,3,2,1,0:T(8,128)(2,1)}, u32[]{:S(2)}) %copy-start) | copy-done | bytes 55320
  2.8 0.2 copy.16
  2.9 0.0 copy-start.3
  2.9 0.2 reshape.23.w3
  3.1 0.7 %copy-done.3 = bf16[32,2,16,128]{3,2,1,0:T(8,128)(2,1)S(1)} copy-done((bf16[32,2,16,128]{3,2,1,0:T(8,128)(2,1)S(1)}, bf16[32,2,16,128]{3,2,1,0:T(8,128)(2,1)}, u32[]{:S(2)}) %copy-start.3) | copy-done | bytes 262168
  3.9 0.0 copy-start.1
  3.9 0.1 copy.19
  4.0 0.8 %copy-done.1 = bf16[3,3,3,32,32]{4,3,2,1,0:T(8,128)(2,1)S(1)} copy-done((bf16[3,3,3,32,32]{4,3,2,1,0:T(8,128)(2,1)S(1)}, bf16[3,3,3,32,32]{4,3,2,1,0:T(8,128)(2,1)}, u32[]{:S(2)}) %copy-start.1) | copy-done | bytes 55320
  4.8 0.1 pad_maximum_fusion
  4.9 0.6 copy.15
  5.5 0.3 reshape.22
  5.8 65.6 %shard_map.76 = (bf16[2,16,32,128]{3,2,1,0:T(8,128)(2,1)S(1)}, f32[864,32]{1,0:T(8,128)S(1)}, f32[864,32]{1,0:T(8,128)S(1)}) custom-call(bf16[2,16,32,128]{3,2,1,0:T(8,128)(2,1)S(1)} %bitcast.15, bf16[64,864]{1,0:T(8,128)(2,1)S(1)} %bitcast.16, bf16[32,1728]{1,0:T(8,128)(2,1)S(1)} %bitcast.17, bf16[32,864]{1,0:T(8,128)(2,1)S(1)} %reshape.23.w3), custom_call_target="tpu_custom_call" | custom-call | tf_op jit(solution)/shard_map/pallas_call | solution.py:366
  71.4 0.8 %copy.17 = bf16[32,2,16,128]{3,2,1,0:T(8,128)(2,1)} copy(bf16[32,2,16,128]{3,0,2,1:T(8,128)(2,1)S(1)} %bitcast.18) | data formatting | bytes 524288
  72.2 0.1 broadcast_multiply_fusion
  72.3 0.0 copy-start.2
  72.3 0.8 %add_multiply_fusion = f32[3,3,3,32,32]{4,3,2,1,0:T(8,128)} fusion(f32[3,3,3,32,32]{4,3,2,1,0:T(8,128)S(1)} %bitcast.20, bf16[3,3,3,32,32]{4,3,2,1,0:T(8,128)(2,1)S(1)} %copy-done.1), kind=kLoop, calls=%fused_computation.1 | loop fusion | flops 110592 | bytes 276480 | tf_op jit(solution)/shard_map/mul | solution.py:408
  73.1 0.1 copy-done.2
  73.2 0.8 %add_multiply_fusion.1 = f32[3,3,3,32,32]{4,3,2,1,0:T(8,128)} fusion(f32[3,3,3,32,32]{4,3,2,1,0:T(8,128)S(1)} %bitcast.19, bf16[3,3,3,32,32]{4,3,2,1,0:T(8,128)(2,1)S(1)} %copy-done.2), kind=kLoop, calls=%fused_computation.2 | loop fusion | flops 110592 | bytes 276480 | tf_op jit(solution)/shard_map/mul | solution.py:407
  (1 shorter events, 0.0 us)
Async XLA Ops:
  1.8 0.9 %copy-start = (bf16[3,3,3,32,32]{4,3,2,1,0:T(8,128)(2,1)S(1)}, bf16[3,3,3,32,32]{4,3,2,1,0:T(8,128)(2,1)}, u32[]{:S(2)}) copy-start(bf16[3,3,3,32,32]{4,3,2,1,0:T(8,128)(2,1)} %param.7) | copy-start | bytes 165892
  2.9 1.0 %copy-start.3 = (bf16[32,2,16,128]{3,2,1,0:T(8,128)(2,1)S(1)}, bf16[32,2,16,128]{3,2,1,0:T(8,128)(2,1)}, u32[]{:S(2)}) copy-start(bf16[32,2,16,128]{3,2,1,0:T(8,128)(2,1)} %param.5) | copy-start | bytes 786436
  3.9 0.9 %copy-start.1 = (bf16[3,3,3,32,32]{4,3,2,1,0:T(8,128)(2,1)S(1)}, bf16[3,3,3,32,32]{4,3,2,1,0:T(8,128)(2,1)}, u32[]{:S(2)}) copy-start(bf16[3,3,3,32,32]{4,3,2,1,0:T(8,128)(2,1)} %param.9) | copy-start | bytes 165892
  72.3 0.9 %copy-start.2 = (bf16[3,3,3,32,32]{4,3,2,1,0:T(8,128)(2,1)S(1)}, bf16[3,3,3,32,32]{4,3,2,1,0:T(8,128)(2,1)}, u32[]{:S(2)}) copy-start(bf16[3,3,3,32,32]{4,3,2,1,0:T(8,128)(2,1)} %param.8) | copy-start | bytes 165892

commit v2 on v1

--- a/solution.py
+++ b/solution.py
@@ -41,7 +41,8 @@
     gv2,
     *scratch,
 ):
-    (rv, rp, rj, zv, zp, zj, ev, ep, ej, sv, sp, slope_ref, back_ref, acc, pack, land, part, full,
+    (rv, rp, rj, zv, zp, zj, ev, ep, ej, sv, sp, sj, slope_ref, back_ref,
+     t1, t2, t3, shift, keep, acc, pack, land, part, full,
      hsend, hrecv, asend, arecv, bsend, brecv) = scratch
     depth, height, chan, width = volume.shape
     me = tuple(lax.axis_index(a) for a in AXES)
@@ -117,13 +118,21 @@
                 ref = landing(step, rows, zbuf)
                 ref[...] = jnp.zeros(ref.shape, ref.dtype)
 
-    def receive(rows, zbuf, edge, slot):
+    def receive(rows, zbuf, edge, slot, kind):
         for step in STEPS:
+            if (step[0] != 0) != (kind == 1):
+                continue
             back = tuple(-d for d in step)
 
             @pl.when(there(back))
             def _():
                 message(step, rows, zbuf, edge, slot).wait_recv()
+
+    def stage(rows, zbuf, edge, slot, out, table, group, finish):
+        for kind in range(2):
+            receive(rows, zbuf, edge, slot, kind)
+            spread(rows, zbuf, out, (near, far)[kind])
+            convolve(table, out, group, kind, finish)
 
     def sent(rows, zbuf, edge, slot):
         for step in STEPS:
@@ -148,57 +157,118 @@
             built = lax.fori_loop(0, height, step, built, unroll=4)
         edge[...] = built.astype(edge.dtype)
 
-    def spread(rows, zbuf, out):
+    def shifter():
+        src = lax.broadcasted_iota(jnp.int32, (2 * width, 2 * width), 0)
+        dst = lax.broadcasted_iota(jnp.int32, (2 * width, 2 * width), 1)
+        cells = depth * height
+        low = jnp.logical_or(
+            jnp.logical_and(src == dst - 1, src < width - 1),
+            jnp.logical_and(
+                dst == 0, jnp.logical_and(src >= width + cells, src < width + 2 * cells)
+            ),
+        )
+        high = jnp.logical_or(
+            jnp.logical_and(src == dst - width + 1, src < width),
+            jnp.logical_and(
+                dst == 2 * width - 1, jnp.logical_and(src >= width, src < width + cells)
+            ),
+        )
+        pick = jnp.logical_or(
+            jnp.logical_and(dst < width, low), jnp.logical_and(dst >= width, high)
+        )
+        shift[...] = jnp.where(pick, 1.0, 0.0).astype(shift.dtype)
+
+    near = tuple(range(1, depth + 1))
+    far = (0, depth + 1)
+
+    def spread(rows, zbuf, out, planes):
         count = rows.shape[2]
         groups = count // chan
         lane = lax.broadcasted_iota(jnp.int32, (count, width), 1)
         cells = depth * height
 
-        def one(xp, yp, dy, y):
+        def block(xp, yp, dy, y, many):
             dx = 0 if xp == 0 else (2 if xp == depth + 1 else 1)
-            at = (xp - 1) % depth * height + y
-            row = rows[xp, yp]
-            wide = row.astype(jnp.float32)
             left = zbuf[0, dx, dy].astype(jnp.float32)
             right = zbuf[1, dx, dy].astype(jnp.float32)
-            low = jnp.where(
-                lane == 0,
-                pltpu.roll(left, width - cells - at, 1),
-                pltpu.roll(wide, 1, 1),
-            ).astype(row.dtype)
-            high = jnp.where(
-                lane == width - 1,
-                pltpu.roll(right, width - 1 - at, 1),
-                pltpu.roll(wide, width - 1, 1),
-            ).astype(row.dtype)
-            for g in range(groups):
-                part_of = slice(g * chan, (g + 1) * chan)
-                base = g * 3 * chan
-                out[xp, yp, base : base + chan] = low[part_of]
-                out[xp, yp, base + chan : base + 2 * chan] = row[part_of]
-                out[xp, yp, base + 2 * chan : base + 3 * chan] = high[part_of]
-
-        for xp in range(depth + 2):
-            one(xp, 0, 0, height - 1)
-            one(xp, height + 1, 2, 0)
-
-            @pl.loop(0, height, unroll=2)
-            def _(y, xp=xp):
-                one(xp, y + 1, 1, y)
-
-    def window(ref, x, y, span):
-        return ref[pl.ds(x, span), pl.ds(y, 3)].reshape(span * 3 * ref.shape[2], width)
-
-    def convolve(weights, ref, finish):
-        for x in range(depth):
-
-            @pl.loop(0, height // 2)
-            def _(j, x=x):
-                y = 2 * j
-                rhs = jnp.concatenate([window(ref, x, y, 3), window(ref, x, y + 1, 3)], axis=1)
-                out = jnp.dot(weights[...], rhs, preferred_element_type=jnp.float32)
-                finish(x, y, out[:, :width])
-                finish(x, y + 1, out[:, width:])
+            halo = []
+            for i in range(many):
+                at = (xp - 1) % depth * height + y + i
+                both = jnp.where(lane == at, right, jnp.where(lane == cells + at, left, 0.0))
+                halo.append(both.astype(rows.dtype))
+            wide = rows[xp, pl.ds(yp, many)].reshape(many * count, width)
+            lhs = jnp.concatenate([wide, jnp.concatenate(halo, axis=0)], axis=1)
+            moved = jnp.dot(lhs, shift[...], preferred_element_type=jnp.float32)
+            moved = moved.astype(rows.dtype)
+            for i in range(many):
+                for g in range(groups):
+                    at = slice(i * count + g * chan, i * count + (g + 1) * chan)
+                    base = g * 3 * chan
+                    out[xp, yp + i, base : base + chan] = moved[at, :width]
+                    out[xp, yp + i, base + chan : base + 2 * chan] = wide[at]
+                    out[xp, yp + i, base + 2 * chan : base + 3 * chan] = moved[at, width:]
+
+        many = 4 // groups
+        for xp in planes:
+            block(xp, 0, 0, height - 1, 1)
+            block(xp, height + 1, 2, 0, 1)
+
+            @pl.loop(0, height // many)
+            def _(j, xp=xp):
+                block(xp, many * j + 1, 1, many * j, many)
+
+    def band(weights, table, group):
+        outs = weights.shape[0]
+        third = weights.shape[1] // 3
+        step = third // 3
+        table[...] = jnp.zeros_like(table)
+        for kx in range(3):
+            piece = weights[:, kx * third : (kx + 1) * third]
+            for ox in range(depth):
+                xp = ox + kx
+                kind, pos = (0, near.index(xp)) if xp in near else (1, far.index(xp))
+                for oy in range(group):
+                    row = (ox * group + oy) * outs
+                    at = (pos * (group + 2) + oy) * step
+                    table[kind, row : row + outs, at : at + third] = piece
+
+    def convolve(table, ref, group, kind, finish):
+        outs = table.shape[1] // (depth * group)
+        planes = (near, far)[kind]
+
+        @pl.loop(0, height // (2 * group))
+        def _(j):
+            halves = []
+            for half in range(2):
+                y = (2 * j + half) * group
+                halves.append(
+                    jnp.concatenate(
+                        [
+                            ref[xp, pl.ds(y, group + 2)].reshape(
+                                (group + 2) * ref.shape[2], width
+                            )
+                            for xp in planes
+                        ],
+                        axis=0,
+                    )
+                )
+            rhs = jnp.concatenate(halves, axis=1)
+            out = jnp.dot(
+                table[kind, :, : rhs.shape[0]], rhs, preferred_element_type=jnp.float32
+            )
+            if kind == 0:
+                keep[j] = out
+                return
+            out = out + keep[j]
+            for half in range(2):
+                for ox in range(depth):
+                    for oy in range(group):
+                        row = (ox * group + oy) * outs
+                        finish(
+                            ox,
+                            (2 * j + half) * group + oy,
+                            out[row : row + outs, half * width : (half + 1) * width],
+                        )
 
     def correlate(ref, rows, offset):
         acc[...] = jnp.zeros_like(acc)
@@ -302,11 +372,12 @@
     for rows, zbuf in ((rv, zv), (rp, zp), (rj, zj)):
         clear(rows, zbuf)
     pl.semaphore_wait(barrier, total - 1)
-
     send(rv, zv, ev, 0, False)
     send(rv, zv, ev, 0, True)
-    receive(rv, zv, ev, 0)
-    spread(rv, zv, sv)
+    shifter()
+    band(w1, t1, 2)
+    band(w2, t2, 4)
+    band(w3, t3, 4)
 
     def first(x, y, out):
         hidden, slope = gelu_pair(out[:chan])
@@ -314,31 +385,26 @@
         rp[x + 1, y + 1, :chan] = hidden.astype(jnp.bfloat16)
         rp[x + 1, y + 1, chan:] = (slope * out[chan:]).astype(jnp.bfloat16)
 
-    convolve(w1, sv, first)
+    stage(rv, zv, ev, 0, sv, t1, 2, first)
     send(rp, zp, ep, 1, False)
     edges(rp, ep)
     send(rp, zp, ep, 1, True)
-    receive(rp, zp, ep, 1)
-    spread(rp, zp, sp)
 
     def second(x, y, out):
         rj[x + 1, y + 1] = out.astype(jnp.bfloat16)
 
-    convolve(w2, sp, second)
+    stage(rp, zp, ep, 1, sp, t2, 4, second)
     send(rj, zj, ej, 2, False)
     edges(rj, ej)
     send(rj, zj, ej, 2, True)
     jv_out[...] = rj[inner]
     correlate(sp, rj, 1)
     scatter(0)
-    receive(rj, zj, ej, 2)
-    sj = sp.at[:, :, : 3 * chan]
-    spread(rj, zj, sj)
 
     def third(x, y, out):
         back_ref[x, y] = (slope_ref[x, y] * out).astype(jnp.bfloat16)
 
-    convolve(w3, sj, third)
+    stage(rj, zj, ej, 2, sj, t3, 4, third)
     gather(0)
     correlate(sv, back_ref, 0)
     scatter(1)
@@ -384,8 +450,14 @@
             pltpu.VMEM((chan, width), bf),
             pltpu.VMEM(pads + (3 * chan, width), bf),
             pltpu.VMEM(pads + (6 * chan, width), bf),
+            pltpu.VMEM(pads + (3 * chan, width), bf),
             pltpu.VMEM((depth, height, chan, width), f32),
             pltpu.VMEM((depth, height, chan, width), bf),
+            pltpu.VMEM((2, depth * 2 * 2 * chan, depth * 4 * 3 * chan), bf),
+            pltpu.VMEM((2, depth * 4 * chan, depth * 6 * 6 * chan), bf),
+            pltpu.VMEM((2, depth * 4 * chan, depth * 6 * 3 * chan), bf),
+            pltpu.VMEM((2 * width, 2 * width), bf),
+            pltpu.VMEM((height // 4, depth * 4 * chan, 2 * width), f32),
             pltpu.VMEM((3, 9 * chan, chan), f32),
             pltpu.VMEM((2, tiles, 8, width), f32),
             pltpu.VMEM((2, total - 1, 8, width), f32),

time: 74.3 us -> 62.8 us (0.85)
  Pallas kernels: 65.6 us -> 54.1 us
    pallas_call x1, Pallas kernels: 65.6 us -> 54.1 us  [body(): pl.pallas_call(functools.partial(kernel, sizes), out_shape=(jax.ShapeDtyp...]
where the time goes in v2:
time: 62.8 us; the launch traced here: 62.5 us
  Pallas kernels  54.1 us (86%)
  local copies, waits for them, and re-layouts  4.74 us (8%)
  other arithmetic  3.02 us (5%)
  between operations  0.71 us (1%)
    pallas_call x1, Pallas kernels, body(): pl.pallas_call(functools.partial(kernel, sizes), out_shape=(jax.ShapeDtyp...  54.1 us
    unnamed x10, local copies, waits for them, and re-layouts  3.37 us

profile of v2, /device:TPU:0, one launch (start us, length us, event | category | flops | bytes accessed | tf_op | source)
XLA Modules:
  0.0 62.5 jit_solution(17769757326140442599)
XLA Ops:
  0.6 1.2 %pad_maximum_fusion.1 = bf16[3,3,3,32,64]{4,3,2,1,0:T(8,128)(2,1)S(1)} fusion(bf16[3,3,3,32,32]{4,3,2,1,0:T(8,128)(2,1)} %param.8, bf16[3,3,3,32,32]{4,3,2,1,0:T(8,128)(2,1)} %param.6), kind=kLoop, calls=%fused_computation.4 | loop fusion | flops 221184 | bytes 221184 | tf_op jit(solution)/shard_map/concatenate | solution.py:425
  1.8 0.0 copy-start
  1.8 0.1 copy.14
  2.0 0.8 %copy-done = bf16[3,3,3,32,32]{4,3,2,1,0:T(8,128)(2,1)S(1)} copy-done((bf16[3,3,3,32,32]{4,3,2,1,0:T(8,128)(2,1)S(1)}, bf16[3,3,3,32,32]{4,3,2,1,0:T(8,128)(2,1)}, u32[]{:S(2)}) %copy-start) | copy-done | bytes 55320
  2.8 0.2 copy.16
  2.9 0.0 copy-start.3
  2.9 0.2 reshape.23.w3
  3.1 0.7 %copy-done.3 = bf16[32,2,16,128]{3,2,1,0:T(8,128)(2,1)S(1)} copy-done((bf16[32,2,16,128]{3,2,1,0:T(8,128)(2,1)S(1)}, bf16[32,2,16,128]{3,2,1,0:T(8,128)(2,1)}, u32[]{:S(2)}) %copy-start.3) | copy-done | bytes 262168
  3.9 0.0 copy-start.1
  3.9 0.1 copy.19
  4.0 0.8 %copy-done.1 = bf16[3,3,3,32,32]{4,3,2,1,0:T(8,128)(2,1)S(1)} copy-done((bf16[3,3,3,32,32]{4,3,2,1,0:T(8,128)(2,1)S(1)}, bf16[3,3,3,32,32]{4,3,2,1,0:T(8,128)(2,1)}, u32[]{:S(2)}) %copy-start.1) | copy-done | bytes 55320
  4.8 0.1 pad_maximum_fusion
  4.9 0.6 copy.15
  5.5 0.3 reshape.22
  5.8 54.1 %shard_map.76 = (bf16[2,16,32,128]{3,2,1,0:T(8,128)(2,1)S(1)}, f32[864,32]{1,0:T(8,128)S(1)}, f32[864,32]{1,0:T(8,128)S(1)}) custom-call(bf16[2,16,32,128]{3,2,1,0:T(8,128)(2,1)S(1)} %bitcast.15, bf16[64,864]{1,0:T(8,128)(2,1)S(1)} %bitcast.16, bf16[32,1728]{1,0:T(8,128)(2,1)S(1)} %bitcast.17, bf16[32,864]{1,0:T(8,128)(2,1)S(1)} %reshape.23.w3), custom_call_target="tpu_custom_call" | custom-call | tf_op jit(solution)/shard_map/pallas_call | solution.py:432
  59.9 0.8 %copy.17 = bf16[32,2,16,128]{3,2,1,0:T(8,128)(2,1)} copy(bf16[32,2,16,128]{3,0,2,1:T(8,128)(2,1)S(1)} %bitcast.18) | data formatting | bytes 524288
  60.7 0.1 broadcast_multiply_fusion
  60.8 0.0 copy-start.2
  60.8 0.8 %add_multiply_fusion = f32[3,3,3,32,32]{4,3,2,1,0:T(8,128)} fusion(f32[3,3,3,32,32]{4,3,2,1,0:T(8,128)S(1)} %bitcast.20, bf16[3,3,3,32,32]{4,3,2,1,0:T(8,128)(2,1)S(1)} %copy-done.1), kind=kLoop, calls=%fused_computation.1 | loop fusion | flops 110592 | bytes 276480 | tf_op jit(solution)/shard_map/mul | solution.py:480
  61.6 0.1 copy-done.2
  61.7 0.8 %add_multiply_fusion.1 = f32[3,3,3,32,32]{4,3,2,1,0:T(8,128)} fusion(f32[3,3,3,32,32]{4,3,2,1,0:T(8,128)S(1)} %bitcast.19, bf16[3,3,3,32,32]{4,3,2,1,0:T(8,128)(2,1)S(1)} %copy-done.2), kind=kLoop, calls=%fused_computation.2 | loop fusion | flops 110592 | bytes 276480 | tf_op jit(solution)/shard_map/mul | solution.py:479
  (1 shorter events, 0.0 us)
Async XLA Ops:
  1.8 0.9 %copy-start = (bf16[3,3,3,32,32]{4,3,2,1,0:T(8,128)(2,1)S(1)}, bf16[3,3,3,32,32]{4,3,2,1,0:T(8,128)(2,1)}, u32[]{:S(2)}) copy-start(bf16[3,3,3,32,32]{4,3,2,1,0:T(8,128)(2,1)} %param.7) | copy-start | bytes 165892
  2.9 1.0 %copy-start.3 = (bf16[32,2,16,128]{3,2,1,0:T(8,128)(2,1)S(1)}, bf16[32,2,16,128]{3,2,1,0:T(8,128)(2,1)}, u32[]{:S(2)}) copy-start(bf16[32,2,16,128]{3,2,1,0:T(8,128)(2,1)} %param.5) | copy-start | bytes 786436
  3.9 0.9 %copy-start.1 = (bf16[3,3,3,32,32]{4,3,2,1,0:T(8,128)(2,1)S(1)}, bf16[3,3,3,32,32]{4,3,2,1,0:T(8,128)(2,1)}, u32[]{:S(2)}) copy-start(bf16[3,3,3,32,32]{4,3,2,1,0:T(8,128)(2,1)} %param.9) | copy-start | bytes 165892
  60.8 0.9 %copy-start.2 = (bf16[3,3,3,32,32]{4,3,2,1,0:T(8,128)(2,1)S(1)}, bf16[3,3,3,32,32]{4,3,2,1,0:T(8,128)(2,1)}, u32[]{:S(2)}) copy-start(bf16[3,3,3,32,32]{4,3,2,1,0:T(8,128)(2,1)} %param.8) | copy-start | bytes 165892

commit v3 on v2

--- a/solution.py
+++ b/solution.py
@@ -36,6 +36,8 @@
     w1,
     w2,
     w3,
+    d1,
+    d2,
     jv_out,
     gv1,
     gv2,
@@ -187,35 +189,27 @@
         lane = lax.broadcasted_iota(jnp.int32, (count, width), 1)
         cells = depth * height
 
-        def block(xp, yp, dy, y, many):
+        for xp in planes:
             dx = 0 if xp == 0 else (2 if xp == depth + 1 else 1)
-            left = zbuf[0, dx, dy].astype(jnp.float32)
-            right = zbuf[1, dx, dy].astype(jnp.float32)
             halo = []
-            for i in range(many):
-                at = (xp - 1) % depth * height + y + i
+            for yp in range(height + 2):
+                dy = 0 if yp == 0 else (2 if yp == height + 1 else 1)
+                left = zbuf[0, dx, dy].astype(jnp.float32)
+                right = zbuf[1, dx, dy].astype(jnp.float32)
+                at = (xp - 1) % depth * height + (yp - 1) % height
                 both = jnp.where(lane == at, right, jnp.where(lane == cells + at, left, 0.0))
                 halo.append(both.astype(rows.dtype))
-            wide = rows[xp, pl.ds(yp, many)].reshape(many * count, width)
+            wide = rows[xp].reshape((height + 2) * count, width)
             lhs = jnp.concatenate([wide, jnp.concatenate(halo, axis=0)], axis=1)
             moved = jnp.dot(lhs, shift[...], preferred_element_type=jnp.float32)
-            moved = moved.astype(rows.dtype)
-            for i in range(many):
-                for g in range(groups):
-                    at = slice(i * count + g * chan, i * count + (g + 1) * chan)
-                    base = g * 3 * chan
-                    out[xp, yp + i, base : base + chan] = moved[at, :width]
-                    out[xp, yp + i, base + chan : base + 2 * chan] = wide[at]
-                    out[xp, yp + i, base + 2 * chan : base + 3 * chan] = moved[at, width:]
-
-        many = 4 // groups
-        for xp in planes:
-            block(xp, 0, 0, height - 1, 1)
-            block(xp, height + 1, 2, 0, 1)
-
-            @pl.loop(0, height // many)
-            def _(j, xp=xp):
-                block(xp, many * j + 1, 1, many * j, many)
+            moved = moved.astype(rows.dtype).reshape(height + 2, count, 2 * width)
+            kept = wide.reshape(height + 2, count, width)
+            for g in range(groups):
+                at = slice(g * chan, (g + 1) * chan)
+                base = g * 3 * chan
+                out[xp, :, base : base + chan] = moved[:, at, :width]
+                out[xp, :, base + chan : base + 2 * chan] = kept[:, at]
+                out[xp, :, base + 2 * chan : base + 3 * chan] = moved[:, at, width:]
 
     def band(weights, table, group):
         outs = weights.shape[0]
@@ -291,6 +285,8 @@
                     acc[kx] += lax.dot_general(lhs, rhs, NT, preferred_element_type=jnp.float32)
 
     tiles = pack.shape[1]
+    cells_all = float(depth * height * width * total)
+    factor = math.sqrt(27.0 * chan)
 
     def owner(t):
         return t * total // tiles
@@ -347,7 +343,7 @@
             held = jnp.logical_or(held, line == owner(t))
         return held
 
-    def drain(slot, out):
+    def drain(slot, out, direction):
         held = owning()
         for flag, count in ((held, tiles - 1), (jnp.logical_not(held), tiles)):
 
@@ -364,7 +360,9 @@
 
         whole = full[slot].reshape(span, width)
         for j in range(lanes):
-            out[j * span : (j + 1) * span] = whole[:, j * chan : (j + 1) * chan]
+            at = slice(j * span, (j + 1) * span)
+            damp = 0.1 * direction[at].astype(jnp.float32)
+            out[at] = factor * (whole[:, j * chan : (j + 1) * chan] / cells_all + damp)
 
     inner = (slice(1, depth + 1), slice(1, height + 1))
     rv[inner] = volume[...]
@@ -409,8 +407,8 @@
     correlate(sv, back_ref, 0)
     scatter(1)
     gather(1)
-    drain(0, gv2)
-    drain(1, gv1)
+    drain(0, gv2, d2)
+    drain(1, gv1, d1)
     sent(rv, zv, ev, 0)
     sent(rp, zp, ep, 1)
     sent(rj, zj, ej, 2)
@@ -436,7 +434,7 @@
             jax.ShapeDtypeStruct((filt, chan), f32),
             jax.ShapeDtypeStruct((filt, chan), f32),
         ),
-        in_specs=[vmem] * 4,
+        in_specs=[vmem] * 6,
         out_specs=(vmem,) * 3,
         scratch_shapes=[
             pltpu.VMEM(pads + (chan, width), bf),
@@ -473,12 +471,12 @@
         compiler_params=pltpu.CompilerParams(
             collective_id=0, has_side_effects=True, vmem_limit_bytes=48 * 1024 * 1024
         ),
-    )(cells, w1, w2, w3)
-    count = float(depth * height * width * total)
-    factor = math.sqrt(27.0 * chan)
-    gv_first = factor * (corr1.reshape(v_first.shape) / count + 0.1 * v_first.astype(f32))
-    gv_second = factor * (corr2.reshape(v_second.shape) / count + 0.1 * v_second.astype(f32))
-    return jnp.transpose(jv, (2, 0, 1, 3)), gv_first, gv_second
+    )(cells, w1, w2, w3, v_first.reshape(filt, chan), v_second.reshape(filt, chan))
+    return (
+        jnp.transpose(jv, (2, 0, 1, 3)),
+        corr1.reshape(v_first.shape),
+        corr2.reshape(v_second.shape),
+    )
 
 
 def solution(mesh):

time: 62.8 us -> 59 us (0.939)
  Pallas kernels: 54.1 us -> 50 us
  local copies, waits for them, and re-layouts: 4.74 us -> 6.81 us
  other arithmetic: 3.02 us -> 1.28 us
    pallas_call x1, Pallas kernels: 54.1 us -> 50 us  [body(): pl.pallas_call(functools.partial(kernel, sizes), out_shape=(jax.ShapeDtyp...]
    unnamed x10 -> x12, local copies, waits for them, and re-layouts: 3.37 us -> 5.43 us
    mul x2 -> x0, other arithmetic: 1.68 us -> none  [the longest x1 0.84 us: body(): factor * (corr2.reshape(v_second.shape) / count + 0.1 * v_second.astype(f...]
where the time goes in v3:
time: 59 us; the launch traced here: 58.8 us
  Pallas kernels  50 us (85%)
  local copies, waits for them, and re-layouts  6.81 us (12%)
  other arithmetic  1.28 us (2%)
  between operations  0.7 us (1%)
    pallas_call x1, Pallas kernels, body(): pl.pallas_call(functools.partial(kernel, sizes), out_shape=(jax.ShapeDtyp...  50 us
    unnamed x12, local copies, waits for them, and re-layouts  5.43 us

profile of v3, /device:TPU:0, one launch (start us, length us, event | category | flops | bytes accessed | tf_op | source)
XLA Modules:
  0.0 58.8 jit_solution(5199614803778285124)
XLA Ops:
  0.6 1.2 %pad_maximum_fusion.1 = bf16[3,3,3,32,64]{4,3,2,1,0:T(8,128)(2,1)S(1)} fusion(bf16[3,3,3,32,32]{4,3,2,1,0:T(8,128)(2,1)} %param.8, bf16[3,3,3,32,32]{4,3,2,1,0:T(8,128)(2,1)} %param.6), kind=kLoop, calls=%fused_computation.2 | loop fusion | flops 221184 | bytes 221184 | tf_op jit(solution)/shard_map/concatenate | solution.py:423
  1.8 0.0 copy-start.2
  1.8 0.1 copy.14
  2.0 0.8 %copy-done.2 = bf16[3,3,3,32,32]{4,3,2,1,0:T(8,128)(2,1)S(1)} copy-done((bf16[3,3,3,32,32]{4,3,2,1,0:T(8,128)(2,1)S(1)}, bf16[3,3,3,32,32]{4,3,2,1,0:T(8,128)(2,1)}, u32[]{:S(2)}) %copy-start.2) | copy-done | bytes 55320
  2.8 0.2 copy.16
  2.9 0.0 copy-start.3
  2.9 0.2 reshape.29.w3
  3.1 0.7 %copy-done.3 = bf16[32,2,16,128]{3,2,1,0:T(8,128)(2,1)S(1)} copy-done((bf16[32,2,16,128]{3,2,1,0:T(8,128)(2,1)S(1)}, bf16[32,2,16,128]{3,2,1,0:T(8,128)(2,1)}, u32[]{:S(2)}) %copy-start.3) | copy-done | bytes 262168
  3.9 0.0 copy-start
  3.9 0.1 copy.19
  4.0 0.8 %copy-done = bf16[3,3,3,32,32]{4,3,2,1,0:T(8,128)(2,1)S(1)} copy-done((bf16[3,3,3,32,32]{4,3,2,1,0:T(8,128)(2,1)S(1)}, bf16[3,3,3,32,32]{4,3,2,1,0:T(8,128)(2,1)}, u32[]{:S(2)}) %copy-start) | copy-done | bytes 55320
  4.8 0.1 pad_maximum_fusion
  4.9 0.6 copy.15
  5.5 0.0 copy-start.1
  5.5 0.3 reshape.28
  5.8 0.6 %copy-done.1 = bf16[3,3,3,32,32]{4,3,2,1,0:T(8,128)(2,1)S(1)} copy-done((bf16[3,3,3,32,32]{4,3,2,1,0:T(8,128)(2,1)S(1)}, bf16[3,3,3,32,32]{4,3,2,1,0:T(8,128)(2,1)}, u32[]{:S(2)}) %copy-start.1) | copy-done | bytes 55320
  6.5 50.0 %shard_map.76 = (bf16[2,16,32,128]{3,2,1,0:T(8,128)(2,1)S(1)}, f32[864,32]{1,0:T(8,128)S(1)}, f32[864,32]{1,0:T(8,128)S(1)}) custom-call(bf16[2,16,32,128]{3,2,1,0:T(8,128)(2,1)S(1)} %bitcast.17, bf16[64,864]{1,0:T(8,128)(2,1)S(1)} %bitcast.21, bf16[32,1728]{1,0:T(8,128)(2,1)S(1)} %bitcast.22, bf16[32,864]{1,0:T(8,128)(2,1)S(1)} %reshape.29.w3, ...), custom_call_target="tpu_custom_call" | custom-call | tf_op jit(solution)/shard_map/pallas_call | solution.py:430
  56.4 0.8 %copy.17 = bf16[32,2,16,128]{3,2,1,0:T(8,128)(2,1)} copy(bf16[32,2,16,128]{3,0,2,1:T(8,128)(2,1)S(1)} %bitcast.25) | data formatting | bytes 524288
  57.3 0.8 %copy.22 = f32[3,3,3,32,32]{4,3,2,1,0:T(8,128)} copy(f32[3,3,3,32,32]{4,3,2,1,0:T(8,128)S(1)} %bitcast.24) | data formatting | bytes 221184
  58.0 0.8 %copy.23 = f32[3,3,3,32,32]{4,3,2,1,0:T(8,128)} copy(f32[3,3,3,32,32]{4,3,2,1,0:T(8,128)S(1)} %bitcast.23) | data formatting | bytes 221184
  (1 shorter events, 0.0 us)
Async XLA Ops:
  1.8 0.9 %copy-start.2 = (bf16[3,3,3,32,32]{4,3,2,1,0:T(8,128)(2,1)S(1)}, bf16[3,3,3,32,32]{4,3,2,1,0:T(8,128)(2,1)}, u32[]{:S(2)}) copy-start(bf16[3,3,3,32,32]{4,3,2,1,0:T(8,128)(2,1)} %param.7) | copy-start | bytes 165892
  2.9 1.0 %copy-start.3 = (bf16[32,2,16,128]{3,2,1,0:T(8,128)(2,1)S(1)}, bf16[32,2,16,128]{3,2,1,0:T(8,128)(2,1)}, u32[]{:S(2)}) copy-start(bf16[32,2,16,128]{3,2,1,0:T(8,128)(2,1)} %param.5) | copy-start | bytes 786436
  3.9 0.9 %copy-start = (bf16[3,3,3,32,32]{4,3,2,1,0:T(8,128)(2,1)S(1)}, bf16[3,3,3,32,32]{4,3,2,1,0:T(8,128)(2,1)}, u32[]{:S(2)}) copy-start(bf16[3,3,3,32,32]{4,3,2,1,0:T(8,128)(2,1)} %param.9) | copy-start | bytes 165892
  5.5 0.9 %copy-start.1 = (bf16[3,3,3,32,32]{4,3,2,1,0:T(8,128)(2,1)S(1)}, bf16[3,3,3,32,32]{4,3,2,1,0:T(8,128)(2,1)}, u32[]{:S(2)}) copy-start(bf16[3,3,3,32,32]{4,3,2,1,0:T(8,128)(2,1)} %param.8) | copy-start | bytes 165892
